TPU v7x, 32 devices: a whole 2x2x4 slice. The times are simulated.
32 devices in a mesh: kgrp: 8 (over z, x), scr: 4 (over y, core).
Axes of the slice: x: 2, y: 2, z: 4, core: 2. Of those that a mesh axis runs over, the one named last changes fastest.
Arguments:
- wave_val: bfloat16 [8, 32, 2048], P('kgrp', None, 'scr'), may hold values from -6 to 6
- wave_con: bfloat16 [8, 32, 2048], P('kgrp', None, 'scr'), may hold values from -6 to 6
- excite: bfloat16 [8, 1024, 16], P('kgrp', 'scr'), may hold values from -6 to 6
- screening: bfloat16 [8, 2048, 2048], P('kgrp', None, 'scr'), may hold values from -9.1552734e-05 to 9.1552734e-05
- pair_count: int32 [8], P('kgrp'), may hold values from 1 to 2, as said below
- pair_kpoint: int32 [8, 2], P('kgrp'), may hold values from 0 to 7
- pair_partner: int32 [8, 2], P('kgrp'), may hold values from 0 to 7
Outputs:
- forward: float32 [8, 2, 1024, 16], P('kgrp', None, 'scr')
- transposed: float32 [8, 2, 1024, 16], P('kgrp', None, 'scr')
Inputs may be any that keep to these rules, and one draw needn't show every extreme that they name: Slot p of screening owner h is live when p < pair_count[h]; in every draw some owner has 2 live slots.
All inputs are finite; a program needn't handle non-finite values.
Results may differ from a plain program's by a relative error of at most 0.0057.
Values may be sent and summed in bfloat16 or wider, within the bound.
No kernel may reach another device: no remote copies, remote signals or barrier semaphores. Data moves between devices by JAX's collectives and lax.ppermute only.
A program may use at most 128 MiB of HBM per device.

v0:
```python
import jax
import jax.numpy as jnp
from jax import lax
from jax.sharding import PartitionSpec as P

PTS_BLK = 128


def body(wave_val, wave_con, excite, screening, pair_count, pair_kpoint, pair_partner):
    slots = pair_kpoint.shape[1]
    role_total = 2 * slots
    roles = jnp.concatenate([pair_kpoint[0], pair_partner[0]])
    nval = wave_val.shape[1]
    ncon = wave_con.shape[1]
    mu_dev = wave_val.shape[2]
    rows_dev = excite.shape[1]
    nexc = excite.shape[2]
    pieces = (
        lax.all_gather(wave_val, "kgrp", axis=0, tiled=True),
        lax.all_gather(wave_con, "kgrp", axis=0, tiled=True),
        lax.all_gather(excite, "kgrp", axis=0, tiled=True),
    )
    pieces_here = pieces[0].shape[0]
    kpoint_ids = jnp.arange(pieces_here, dtype=jnp.int32)
    picker = (roles[:, None] == kpoint_ids[None, :]).astype(jnp.bfloat16)
    picked = tuple(
        (
            jnp.dot(picker, piece.reshape(pieces_here, -1), preferred_element_type=jnp.float32)
            for piece in pieces
        )
    )
    sel_val = picked[0].astype(jnp.bfloat16).reshape(role_total, nval, mu_dev)
    sel_con = picked[1].astype(jnp.bfloat16).reshape(role_total, ncon, mu_dev)
    sel_exc = picked[2].astype(jnp.bfloat16).reshape(role_total, rows_dev, nexc)
    full_con, full_exc = (
        lax.all_gather(sel_con, "scr", axis=2, tiled=True),
        lax.all_gather(sel_exc, "scr", axis=1, tiled=True),
    )
    weights = screening[0]
    width_all = full_con.shape[2]
    mu_step = min(width_all, 512)
    mu_blocks = width_all // mu_step
    blocks = mu_dev // PTS_BLK
    ahead_list = []
    back_list = []
    for slot_index in range(slots):
        con_first = full_con[slot_index]
        con_second = full_con[slots + slot_index]
        screen_sum = jnp.zeros((ncon * ncon, mu_dev), jnp.float32)
        for part_index in range(mu_blocks):
            lower = part_index * mu_step
            upper = lower + mu_step
            left = con_first[:, lower:upper].astype(jnp.float32)
            right = con_second[:, lower:upper].astype(jnp.float32)
            density = (
                (left[:, None, :] * right[None, :, :])
                .astype(jnp.bfloat16)
                .reshape(ncon * ncon, mu_step)
            )
            screen_sum = screen_sum + jnp.dot(
                density, weights[lower:upper], preferred_element_type=jnp.float32
            )
        screened = screen_sum.astype(jnp.bfloat16)
        val_first = sel_val[slot_index].astype(jnp.float32)
        val_second = sel_val[slots + slot_index].astype(jnp.float32)
        rho_val = (
            (val_first.T[:, :, None] * val_second.T[:, None, :])
            .astype(jnp.bfloat16)
            .reshape(mu_dev, nval * nval)
        )
        exc_first = full_exc[slot_index].reshape(nval, ncon, nexc)
        exc_second = full_exc[slots + slot_index].reshape(nval, ncon, nexc)
        ahead = jnp.zeros((nval, ncon, nexc), jnp.float32)
        back = jnp.zeros((nval, ncon, nexc), jnp.float32)
        for block_index in range(blocks):
            lower = block_index * PTS_BLK
            upper = lower + PTS_BLK
            kernel = jnp.dot(
                screened[:, lower:upper], rho_val[lower:upper], preferred_element_type=jnp.float32
            )
            kernel = kernel.astype(jnp.bfloat16).reshape(ncon, ncon, nval, nval)
            ahead = ahead + jnp.einsum(
                "cdvw,wde->vce", kernel, exc_second, preferred_element_type=jnp.float32
            )
            back = back + jnp.einsum(
                "cdvw,vce->wde", kernel, exc_first, preferred_element_type=jnp.float32
            )
        ahead_list.append(ahead.reshape(nval * ncon, nexc))
        back_list.append(back.reshape(nval * ncon, nexc))
    ahead_all = jnp.stack(ahead_list)[None]
    back_all = jnp.stack(back_list)[None]
    ahead_own, back_own = (
        lax.psum_scatter(ahead_all, "scr", scatter_dimension=2, tiled=True),
        lax.psum_scatter(back_all, "scr", scatter_dimension=2, tiled=True),
    )
    live = (jnp.arange(slots, dtype=jnp.int32) < pair_count[0]).astype(jnp.float32)[
        None, :, None, None
    ]
    return (ahead_own * live, back_own * live)


def solution(mesh):
    return jax.shard_map(
        body,
        mesh=mesh,
        in_specs=(
            P("kgrp", None, "scr"),
            P("kgrp", None, "scr"),
            P("kgrp", "scr", None),
            P("kgrp", None, "scr"),
            P("kgrp"),
            P("kgrp", None),
            P("kgrp", None),
        ),
        out_specs=(P("kgrp", None, "scr", None), P("kgrp", None, "scr", None)),
        check_vma=False,
    )
```

profile of v0, /device:TPU:0, one launch (start us, length us, event | category | flops | bytes accessed | tf_op | source)
XLA Modules:
  0.0 336.0 jit_solution(14860599294428751384)
XLA Ops:
  7.2 32.6 %all_gather.15 = bf16[8,256,16]{1,2,0:T(8,128)(2,1)S(1)} all-gather(bf16[1,256,16]{1,2,0:T(8,128)(2,1)} %param.9), channel_id=1, replica_groups=mesh['kgrp'=8,'scr'=4] {'kgrp'}, dimensions={0}, use_global_device_ids=true | all-gather | bytes 73728 | tf_op jit(solution)/shard_map/all_gather | solution.py:21
  39.8 30.9 %all_gather.19 = bf16[8,32,512]{2,1,0:T(8,128)(2,1)S(1)} all-gather(bf16[1,32,512]{2,1,0:T(8,128)(2,1)} %param.7), channel_id=1, replica_groups=mesh['kgrp'=8,'scr'=4] {'kgrp'}, dimensions={0}, use_global_device_ids=true | all-gather | bytes 294912 | tf_op jit(solution)/shard_map/all_gather | solution.py:19
  72.7 30.7 %all_gather.17 = bf16[8,32,512]{2,1,0:T(8,128)(2,1)S(1)} all-gather(bf16[1,32,512]{2,1,0:T(8,128)(2,1)S(1)} %copy-done.4), channel_id=1, replica_groups=mesh['kgrp'=8,'scr'=4] {'kgrp'}, dimensions={0}, use_global_device_ids=true | all-gather | bytes 294912 | tf_op jit(solution)/shard_map/all_gather | solution.py:20
  103.9 7.2 %all_gather.18 = bf16[4,32,2048]{2,1,0:T(8,128)(2,1)S(1)} all-gather(bf16[4,32,512]{2,1,0:T(8,128)(2,1)S(1)} %bitcast.303), channel_id=1, replica_groups=mesh['kgrp'=8,'scr'=4] {'scr'}, dimensions={2}, use_global_device_ids=true | all-gather | bytes 655360 | tf_op jit(solution)/shard_map/all_gather | solution.py:36
  112.7 10.4 %all_gather.16 = bf16[4,1024,16]{2,1,0:T(8,128)(2,1)S(1)} all-gather(bf16[4,256,16]{2,1,0:T(8,128)(2,1)S(1)} %reshape.207), channel_id=1, replica_groups=mesh['kgrp'=8,'scr'=4] {'scr'}, dimensions={1}, use_global_device_ids=true | all-gather | bytes 163840 | tf_op jit(solution)/shard_map/all_gather | solution.py:37
  134.2 2.1 convolution_convert_fusion.8
  138.3 2.1 convolution_convert_fusion.10
  143.4 2.0 convolution_convert_fusion.4
  145.4 2.1 convolution_convert_fusion.5
  147.5 2.0 convolution_convert_fusion.6
  149.5 11.4 %reshape.215 = bf16[32,32,32,32]{3,2,1,0:T(8,128)(2,1)} reshape(bf16[1024,1024]{1,0:T(8,128)(2,1)} %convolution_convert_fusion.6) | data formatting | bytes 4194304 | tf_op jit(solution)/shard_map/reshape | solution.py:81
  161.0 10.9 %reshape.216 = bf16[32,32,32,32]{3,2,1,0:T(8,128)(2,1)} reshape(bf16[1024,1024]{1,0:T(8,128)(2,1)} %convolution_convert_fusion.5) | data formatting | bytes 4194304 | tf_op jit(solution)/shard_map/reshape | solution.py:81
  171.9 10.9 %reshape.217 = bf16[32,32,32,32]{3,2,1,0:T(8,128)(2,1)} reshape(bf16[1024,1024]{1,0:T(8,128)(2,1)} %convolution_convert_fusion.4) | data formatting | bytes 4194304 | tf_op jit(solution)/shard_map/reshape | solution.py:81
  182.8 5.9 %convolution_bitcast_fusion.10 = f32[16,32,32]{2,0,1:T(8,128)S(1)} fusion(bf16[32,32,32,32]{3,2,1,0:T(8,128)(2,1)} %reshape.216, bf16[32,32,16]{0,2,1:T(8,128)(2,1)S(1)} %copy.62), kind=kOutput, calls=%fused_computation.33 | convolution fusion | flops 33554432 | bytes 2195456 | tf_op jit(solution)/shard_map/cdvw,wde->vce/dot_general | solution.py:82
  188.7 2.5 convolution_bitcast_fusion.9
  191.2 11.0 %reshape.218 = bf16[32,32,32,32]{3,2,1,0:T(8,128)(2,1)} reshape(bf16[1024,1024]{1,0:T(8,128)(2,1)} %convolution_convert_fusion.3) | data formatting | bytes 4194304 | tf_op jit(solution)/shard_map/reshape | solution.py:81
  202.2 5.8 %convolution_bitcast_fusion.8 = f32[16,32,32]{2,0,1:T(8,128)S(1)} fusion(bf16[32,32,32,32]{3,2,1,0:T(8,128)(2,1)} %reshape.218, bf16[32,32,16]{0,2,1:T(8,128)(2,1)S(1)} %copy.62), kind=kOutput, calls=%fused_computation.31 | convolution fusion | flops 33554432 | bytes 2195456 | tf_op jit(solution)/shard_map/cdvw,wde->vce/dot_general | solution.py:82
  208.0 5.8 %fusion.7 = f32[32,32,16]{0,2,1:T(8,128)S(1)} fusion(f32[16,32,32]{2,0,1:T(8,128)S(1)} %convolution_bitcast_fusion.8, f32[16,32,32]{2,0,1:T(8,128)S(1)} %convolution_bitcast_fusion.9, f32[16,32,32]{2,0,1:T(8,128)S(1)} %convolution_bitcast_fusion.10, bf16[32,32,32,32]{3,2,1,0:T(8,128)(2,1)} %reshape.215, bf16[32,32,16]{0,2,1:T(8,128)(2,1)S(1)} %copy.62), kind=kOutput, calls=%fused_computation.46 | convolution fusion | flops 33603584 | bytes 2392064 | tf_op jit(solution)/shard_map/cdvw,wde->vce/dot_general | solution.py:82
  214.1 10.9 %reshape.211 = bf16[32,32,32,32]{3,2,1,0:T(8,128)(2,1)} reshape(bf16[1024,1024]{1,0:T(8,128)(2,1)} %convolution_convert_fusion.10) | data formatting | bytes 4194304 | tf_op jit(solution)/shard_map/reshape | solution.py:81
  225.0 10.9 %reshape.212 = bf16[32,32,32,32]{3,2,1,0:T(8,128)(2,1)} reshape(bf16[1024,1024]{1,0:T(8,128)(2,1)} %convolution_convert_fusion.9) | data formatting | bytes 4194304 | tf_op jit(solution)/shard_map/reshape | solution.py:81
  235.8 11.1 %reshape.213 = bf16[32,32,32,32]{3,2,1,0:T(8,128)(2,1)} reshape(bf16[1024,1024]{1,0:T(8,128)(2,1)} %convolution_convert_fusion.8) | data formatting | bytes 4194304 | tf_op jit(solution)/shard_map/reshape | solution.py:81
  246.9 5.9 %convolution_bitcast_fusion.14 = f32[16,32,32]{2,0,1:T(8,128)S(1)} fusion(bf16[32,32,32,32]{3,2,1,0:T(8,128)(2,1)} %reshape.212, bf16[32,32,16]{0,2,1:T(8,128)(2,1)S(1)} %copy.56), kind=kOutput, calls=%fused_computation.37 | convolution fusion | flops 33554432 | bytes 2195456 | tf_op jit(solution)/shard_map/cdvw,wde->vce/dot_general | solution.py:82
  252.8 2.5 convolution_bitcast_fusion.13
  255.3 7.9 %reshape.214 = bf16[32,32,32,32]{3,2,1,0:T(8,128)(2,1)} reshape(bf16[1024,1024]{1,0:T(8,128)(2,1)S(1)} %convolution_convert_fusion.7) | data formatting | bytes 4194304 | tf_op jit(solution)/shard_map/reshape | solution.py:81
  263.2 5.7 %convolution_bitcast_fusion.12 = f32[16,32,32]{2,0,1:T(8,128)S(1)} fusion(bf16[32,32,32,32]{3,2,1,0:T(8,128)(2,1)} %reshape.214, bf16[32,32,16]{0,2,1:T(8,128)(2,1)S(1)} %copy.56), kind=kOutput, calls=%fused_computation.35 | convolution fusion | flops 33554432 | bytes 2195456 | tf_op jit(solution)/shard_map/cdvw,wde->vce/dot_general | solution.py:82
  269.0 5.8 %fusion.3 = f32[32,32,16]{0,2,1:T(8,128)S(1)} fusion(f32[16,32,32]{2,0,1:T(8,128)S(1)} %convolution_bitcast_fusion.12, f32[16,32,32]{2,0,1:T(8,128)S(1)} %convolution_bitcast_fusion.13, f32[16,32,32]{2,0,1:T(8,128)S(1)} %convolution_bitcast_fusion.14, bf16[32,32,32,32]{3,2,1,0:T(8,128)(2,1)} %reshape.211, bf16[32,32,16]{0,2,1:T(8,128)(2,1)S(1)} %copy.56), kind=kOutput, calls=%fused_computation.42 | convolution fusion | flops 33603584 | bytes 2392064 | tf_op jit(solution)/shard_map/cdvw,wde->vce/dot_general | solution.py:82
  276.5 5.0 %convolution_bitcast_fusion.2 = f32[16,32,32]{2,0,1:T(8,128)S(1)} fusion(bf16[32,32,32,32]{3,2,1,0:T(8,128)(2,1)} %reshape.216, bf16[32,32,16]{0,2,1:T(8,128)(2,1)S(1)} %copy.78), kind=kOutput, calls=%fused_computation.25 | convolution fusion | flops 33554432 | bytes 2195456 | tf_op jit(solution)/shard_map/cdvw,vce->wde/dot_general | solution.py:85
  281.5 5.0 %convolution_bitcast_fusion.1 = f32[16,32,32]{2,0,1:T(8,128)S(1)} fusion(bf16[32,32,32,32]{3,2,1,0:T(8,128)(2,1)} %reshape.217, bf16[32,32,16]{0,2,1:T(8,128)(2,1)S(1)} %copy.78), kind=kOutput, calls=%fused_computation.24 | convolution fusion | flops 33554432 | bytes 2195456 | tf_op jit(solution)/shard_map/cdvw,vce->wde/dot_general | solution.py:85
  288.3 4.8 %convolution_bitcast_fusion.6 = f32[16,32,32]{2,0,1:T(8,128)S(1)} fusion(bf16[32,32,32,32]{3,2,1,0:T(8,128)(2,1)} %reshape.212, bf16[32,32,16]{0,2,1:T(8,128)(2,1)S(1)} %copy.68), kind=kOutput, calls=%fused_computation.29 | convolution fusion | flops 33554432 | bytes 2195456 | tf_op jit(solution)/shard_map/cdvw,vce->wde/dot_general | solution.py:85
  293.2 5.0 %convolution_bitcast_fusion.5 = f32[16,32,32]{2,0,1:T(8,128)S(1)} fusion(bf16[32,32,32,32]{3,2,1,0:T(8,128)(2,1)} %reshape.213, bf16[32,32,16]{0,2,1:T(8,128)(2,1)S(1)} %copy.68), kind=kOutput, calls=%fused_computation.28 | convolution fusion | flops 33554432 | bytes 2195456 | tf_op jit(solution)/shard_map/cdvw,vce->wde/dot_general | solution.py:85
  298.2 5.0 %convolution_bitcast_fusion.4 = f32[16,32,32]{2,0,1:T(8,128)S(1)} fusion(bf16[32,32,32,32]{3,2,1,0:T(8,128)(2,1)} %reshape.214, bf16[32,32,16]{0,2,1:T(8,128)(2,1)S(1)} %copy.68), kind=kOutput, calls=%fused_computation.27 | convolution fusion | flops 33554432 | bytes 2195456 | tf_op jit(solution)/shard_map/cdvw,vce->wde/dot_general | solution.py:85
  308.1 19.3 %reduce-scatter.5.cloned.1.call-done = f32[1,2,256,16]{2,3,1,0:T(8,128)} async-done(((f32[1,2,1024,16]{2,3,1,0:T(8,128)}), f32[1,2,256,16]{2,3,1,0:T(8,128)}) %reduce-scatter.5.cloned.1.call-update) | async-done | bytes 32784 | tf_op jit(solution)/shard_map/reduce_scatter | solution.py:94
  (91 shorter events, 29.3 us)
Async XLA Ops:
  7.2 65.6 %copy-start.4 = (bf16[1,32,512]{2,1,0:T(8,128)(2,1)S(1)}, bf16[1,32,512]{2,1,0:T(8,128)(2,1)}, u32[]{:S(2)}) copy-start(bf16[1,32,512]{2,1,0:T(8,128)(2,1)} %param.8) | copy-start | bytes 98308
  7.2 300.9 %reduce-scatter.3.cloned.1.call-start = ((), (), s32[]{:S(2)}) async-start(), calls=%async_computation.2 | async-start | bytes 163840 | tf_op jit(solution)/shard_map/reduce_scatter | solution.py:93
  125.3 1.6 copy-start.2
  182.8 5.9 %copy-start = (bf16[32,32,32,32]{3,2,1,0:T(8,128)(2,1)S(1)}, bf16[32,32,32,32]{3,2,1,0:T(8,128)(2,1)}, u32[]{:S(2)}) copy-start(bf16[32,32,32,32]{3,2,1,0:T(8,128)(2,1)} %reshape.217) | copy-start | bytes 6291460
  246.9 5.9 %copy-start.1 = (bf16[32,32,32,32]{3,2,1,0:T(8,128)(2,1)S(1)}, bf16[32,32,32,32]{3,2,1,0:T(8,128)(2,1)}, u32[]{:S(2)}) copy-start(bf16[32,32,32,32]{3,2,1,0:T(8,128)(2,1)} %reshape.213) | copy-start | bytes 6291460
  269.0 7.2 %copy-start.3 = (bf16[1,1024,16]{2,1,0:T(8,128)(2,1)S(1)}, bf16[1,1024,16]{2,1,0:T(8,128)(2,1)}, u32[]{:S(2)}) copy-start(bf16[1,1024,16]{2,1,0:T(8,128)(2,1)} %get-tuple-element.7) | copy-start | bytes 98308
  275.8 51.6 %reduce-scatter.5.cloned.1.call-start = ((), (), s32[]{:S(2)}) async-start(), calls=%async_computation.3 | async-start | bytes 163840 | tf_op jit(solution)/shard_map/reduce_scatter | solution.py:94
  276.5 10.0 %slice-start.4 = ((s8[8388608]{0:T(1024)(128)(4,1)}), s8[4194304]{0:T(1024)(128)(4,1)S(1)}, s32[]{:S(2)}) async-start(s8[8388608]{0:T(1024)(128)(4,1)} %bitcast.277), calls=%async_computation.8 | async-start | bytes 8388608
  281.5 5.1 %slice-start.5 = ((s8[8388608]{0:T(1024)(128)(4,1)}), s8[4194304]{0:T(1024)(128)(4,1)S(1)}, s32[]{:S(2)}) async-start(s8[8388608]{0:T(1024)(128)(4,1)} %bitcast.277), calls=%async_computation.9 | async-start | bytes 8388608
  293.1 10.0 %slice-start = ((s8[8388608]{0:T(1024)(128)(4,1)}), s8[4194304]{0:T(1024)(128)(4,1)S(1)}, s32[]{:S(2)}) async-start(s8[8388608]{0:T(1024)(128)(4,1)} %bitcast.273), calls=%async_computation.4 | async-start | bytes 8388608
  293.2 11.5 %slice-start.2 = ((s8[8388608]{0:T(1024)(128)(4,1)}), s8[4194304]{0:T(1024)(128)(4,1)S(1)}, s32[]{:S(2)}) async-start(s8[8388608]{0:T(1024)(128)(4,1)} %bitcast.275), calls=%async_computation.6 | async-start | bytes 8388608
  298.2 5.0 %slice-start.1 = ((s8[8388608]{0:T(1024)(128)(4,1)}), s8[4194304]{0:T(1024)(128)(4,1)S(1)}, s32[]{:S(2)}) async-start(s8[8388608]{0:T(1024)(128)(4,1)} %bitcast.273), calls=%async_computation.5 | async-start | bytes 8388608
  298.2 6.5 %slice-start.3 = ((s8[8388608]{0:T(1024)(128)(4,1)}), s8[4194304]{0:T(1024)(128)(4,1)S(1)}, s32[]{:S(2)}) async-start(s8[8388608]{0:T(1024)(128)(4,1)} %bitcast.275), calls=%async_computation.7 | async-start | bytes 8388608
Sparse Core Ops, SparseCore 0:
  275.9 19.8 reduce-scatter.2
  307.5 19.8 reduce-scatter.4
where the time goes:
time: 341 us; the launch traced here: 336 us
  blocking collectives  112 us (33%)
  local copies, waits for them, and re-layouts  91.5 us (27%)
  matrix products  90.7 us (27%)
  waiting for transfers between devices  19.4 us (6%)
  between operations  15.3 us (4%)
  other arithmetic  6.93 us (2%)
    reshape x8, local copies, waits for them, and re-layouts, body(): kernel = kernel.astype(jnp.bfloat16).reshape(ncon, ncon, nval, nval)  85 us
    dot_general x8, matrix products, body(): jnp.einsum('cdvw,wde->vce', kernel, exc_second, preferred_element_type=jn...  39.9 us
    all_gather x1, blocking collectives, body(): lax.all_gather(excite, 'kgrp', axis=0, tiled=True)  32.6 us
    all_gather x1, blocking collectives, body(): lax.all_gather(wave_val, 'kgrp', axis=0, tiled=True)  30.9 us
    all_gather x1, blocking collectives, body(): lax.all_gather(wave_con, 'kgrp', axis=0, tiled=True)  30.7 us
    dot_general x8, matrix products, body(): jnp.einsum('cdvw,vce->wde', kernel, exc_first, preferred_element_type=jnp...  29.2 us
    reduce_scatter x1, waiting for transfers between devices, body(): lax.psum_scatter(back_all, 'scr', scatter_dimension=2, tiled=True)  19.3 us
    dot_general x8, matrix products, body(): jnp.dot(screened[:, lower:upper], rho_val[lower:upper], preferred_element...  15.1 us
  transfers between devices with their start and end apart: 2, of which 1 were waited for; matrix products, arithmetic and copies ran while one was open for 9% of the time, Pallas kernels for 0%

commit v1 on v0

v1 whole, which is shorter than its diff:
```python
import functools

import jax
import jax.numpy as jnp
from jax import lax
from jax.experimental import pallas as pl
from jax.experimental.pallas import tpu as pltpu
from jax.sharding import PartitionSpec as P

LANES = 128
F32 = jnp.float32
BF16 = jnp.bfloat16


def pick_kernel(rows, roles_ref, all_ref, out_ref):
    for i in range(out_ref.shape[0]):
        out_ref[i] = all_ref[roles_ref[i], :rows, :]


def nt(a, b):
    return lax.dot_general(a, b, (((1,), (1,)), ((), ())), preferred_element_type=F32)


def pair_products(outer, inner, out_ref, column):
    width = inner.shape[1]
    count = inner.shape[0]
    for i in range(outer.shape[0]):
        out_ref[i * count : (i + 1) * count, column : column + width] = (
            outer[i : i + 1, :] * inner
        ).astype(BF16)


def spread_blocks(kernel, out_ref, group):
    block = kernel.shape[0] // group
    tile = out_ref.shape[1] // group
    for i in range(group):
        for q in range(kernel.shape[1] // tile):
            out_ref[q * block : (q + 1) * block, i * tile : (i + 1) * tile] = kernel[
                i * block : (i + 1) * block, q * tile : (q + 1) * tile
            ]


def main_kernel(
    sizes, roles_ref, gath_ref, all_ref, weights_ref, out_ref,
    rho_ref, vals_ref, screened_ref, spread_ref, vec_ref, diag_ref,
):
    slots, nval, ncon, nexc = sizes
    shards = gath_ref.shape[0]
    mu_dev = weights_ref.shape[1]
    rows_dev = nval * ncon // shards
    exc_rows = nexc * rows_dev // mu_dev
    per = LANES // nexc
    val_at = ncon + exc_rows
    lane = lax.broadcasted_iota(jnp.int32, (per * nval, LANES), 1)
    row = lax.broadcasted_iota(jnp.int32, (per * nval, LANES), 0)
    mask = (row // nval == lane // nexc).astype(BF16)
    e_row = lax.broadcasted_iota(jnp.int32, (nexc, LANES), 0)
    e_lane = lax.broadcasted_iota(jnp.int32, (nexc, LANES), 1)
    repeat = (e_lane % nexc == e_row).astype(BF16)
    for p in range(slots):
        for s in range(shards):
            pair_products(
                gath_ref[s, slots + p, :ncon, :].astype(F32),
                gath_ref[s, p, :ncon, :].astype(F32),
                rho_ref, s * mu_dev,
            )
        screened_ref[...] = jnp.dot(
            rho_ref[...], weights_ref[...], preferred_element_type=F32
        ).astype(BF16)
        pair_products(
            all_ref[roles_ref[p], val_at : val_at + nval, :].astype(F32),
            all_ref[roles_ref[slots + p], val_at : val_at + nval, :].astype(F32),
            vals_ref, 0,
        )
        for way in range(2):
            who = slots + p if way == 0 else p
            for s in range(shards):
                part = gath_ref[s, who, ncon:val_at, :]
                flip = jnp.concatenate(
                    [part[:, i * rows_dev : (i + 1) * rows_dev] for i in range(mu_dev // rows_dev)], axis=0
                )
                vec_ref[s * rows_dev : (s + 1) * rows_dev, :] = lax.dot_general(
                    flip, repeat, (((0,), (0,)), ((), ())), preferred_element_type=F32
                )
            if way == 0:
                kernel = nt(screened_ref[...], vals_ref[...]).astype(BF16)
                count, length = ncon, nval
            else:
                kernel = nt(vals_ref[...], screened_ref[...]).astype(BF16)
                count, length = nval, ncon
            spread_blocks(kernel, spread_ref, count)
            for i in range(count):
                if way == 0:
                    vec = vec_ref[pl.ds(i, length, stride=count), :]
                else:
                    vec = vec_ref[i * length : (i + 1) * length, :]
                vec = vec.astype(BF16)
                tile = per * length
                diag_ref[i * tile : (i + 1) * tile, :] = (
                    jnp.concatenate([vec] * per, axis=0) * mask
                )
            total = jnp.dot(spread_ref[...], diag_ref[...], preferred_element_type=F32).astype(BF16)
            parts = out_ref.shape[0]
            if way == 0:
                for s in range(parts):
                    out_ref[s, p, way] = total[s * ncon : (s + 1) * ncon, :]
            else:
                total = total.reshape(ncon // per, parts, nval // parts, LANES)
                for s in range(parts):
                    out_ref[s, p, way] = total[:, s].reshape(ncon, LANES)


def body(wave_val, wave_con, excite, screening, pair_count, pair_kpoint, pair_partner):
    groups = lax.axis_size("kgrp")
    shards = lax.axis_size("scr")
    slots = pair_kpoint.shape[1]
    nval, mu_dev = wave_val.shape[1:]
    ncon = wave_con.shape[1]
    rows_dev, nexc = excite.shape[1:]
    roles = jnp.concatenate([pair_kpoint[0], pair_partner[0]])
    flip = excite[0].T
    step = mu_dev // rows_dev
    exc_rows = nexc // step
    packed = jnp.concatenate(
        [flip[i * exc_rows : (i + 1) * exc_rows] for i in range(step)], axis=1
    )
    mine = jnp.concatenate([wave_con[0], packed, wave_val[0]], axis=0)
    everyone = lax.all_to_all(
        jnp.broadcast_to(mine[None], (groups,) + mine.shape), "kgrp", 0, 0, tiled=True
    )
    keep = ncon + exc_rows
    vmem = pl.BlockSpec(memory_space=pltpu.VMEM)
    smem = pl.BlockSpec(memory_space=pltpu.SMEM)
    selected = pl.pallas_call(
        functools.partial(pick_kernel, keep),
        out_shape=jax.ShapeDtypeStruct((2 * slots, keep, mu_dev), BF16),
        in_specs=[smem, vmem],
        out_specs=vmem,
    )(roles, everyone)
    gathered = lax.all_gather(selected, "scr", axis=0, tiled=False)
    npb = nval * ncon
    per = LANES // nexc
    parts = nval // per
    split = shards // parts
    partial = pl.pallas_call(
        functools.partial(main_kernel, (slots, nval, ncon, nexc)),
        out_shape=jax.ShapeDtypeStruct((parts, slots, 2, ncon, LANES), BF16),
        in_specs=[smem, vmem, vmem, vmem],
        out_specs=vmem,
        scratch_shapes=[
            pltpu.VMEM((npb, shards * mu_dev), BF16),
            pltpu.VMEM((npb, mu_dev), BF16),
            pltpu.VMEM((npb, mu_dev), BF16),
            pltpu.VMEM((npb // per, npb * per), BF16),
            pltpu.VMEM((npb, LANES), F32),
            pltpu.VMEM((npb * per, LANES), BF16),
        ],
        compiler_params=pltpu.CompilerParams(vmem_limit_bytes=48 * 2**20),
    )(roles, gathered, everyone, screening[0])
    ahead = partial[:, :, 0].reshape(parts, slots, ncon, split, per // split, nexc)
    ahead = ahead.transpose(0, 3, 1, 2, 4, 5).reshape(shards, slots, -1)
    back = partial[:, :, 1].reshape(parts, slots, ncon // per, split, per // split, LANES)
    back = back.transpose(0, 3, 1, 2, 4, 5).reshape(shards, slots, -1)
    if split == 1:
        sent = partial
    else:
        sent = jnp.stack([ahead, back], axis=2)
    taken = lax.all_to_all(sent, "scr", 0, 0, tiled=True)
    summed = jnp.sum(taken.astype(F32), axis=0)
    live = (jnp.arange(slots, dtype=jnp.int32) < pair_count[0]).astype(F32)
    summed = summed * live.reshape((slots,) + (1,) * (summed.ndim - 1))
    few = per // split
    ahead = summed[:, 0].reshape(slots, ncon, few, nexc).transpose(0, 2, 1, 3)
    back = summed[:, 1].reshape(slots, ncon // per, few, per, nexc).transpose(0, 2, 1, 3, 4)
    shape = (1, slots, rows_dev, nexc)
    return ahead.reshape(shape), back.reshape(shape)


def solution(mesh):
    return jax.shard_map(
        body,
        mesh=mesh,
        in_specs=(
            P("kgrp", None, "scr"),
            P("kgrp", None, "scr"),
            P("kgrp", "scr", None),
            P("kgrp", None, "scr"),
            P("kgrp"),
            P("kgrp", None),
            P("kgrp", None),
        ),
        out_specs=(P("kgrp", None, "scr", None), P("kgrp", None, "scr", None)),
        check_vma=False,
    )
```

time: 341 us -> 62.7 us (0.18); the launches traced: 336 us -> 62.2 us
  blocking collectives: 112 us -> 8.11 us
  matrix products: 90.7 us -> 0 us
  local copies, waits for them, and re-layouts: 91.5 us -> 5.96 us
  Pallas kernels: 0 us -> 15.5 us
  between operations: 15.3 us -> 1.34 us
  starting transfers between devices: 0.33 us -> 10.6 us
  other arithmetic: 6.93 us -> 2.14 us
    all_gather x5 -> x1, blocking collectives: 112 us -> 8.11 us  [body(): gathered = lax.all_gather(selected, 'scr', axis=0, tiled=False)]
    dot_general x35 -> x0, matrix products: 90.7 us -> none  [the longest x8 39.9 us: body(): jnp.einsum('cdvw,wde->vce', kernel, exc_second, preferred_element_type=jn...]
    reshape x10 -> x1, local copies, waits for them, and re-layouts: 86 us -> 0.71 us  [body(): return (ahead.reshape(shape), back.reshape(shape))]
    reduce_scatter x2 -> x0, waiting for transfers between devices: 19.3 us -> none  [the longest x1 19.3 us: body(): lax.psum_scatter(back_all, 'scr', scatter_dimension=2, tiled=True)]
    all_to_all x0 -> x2, waiting for transfers between devices: none -> 18.5 us  [the longest x1 14 us: body(): lax.all_to_all(jnp.broadcast_to(mine[None], (groups,) + mine.shape), 'kgr...]
    pallas_call x0 -> x2, Pallas kernels: none -> 15.5 us  [the longest x1 13.8 us: body(): pl.pallas_call(functools.partial(main_kernel, (slots, nval, ncon, nexc)),...]
    all_to_all x0 -> x2, starting transfers between devices: none -> 10.6 us  [the longest x1 7.28 us: body(): lax.all_to_all(jnp.broadcast_to(mine[None], (groups,) + mine.shape), 'kgr...]
  transfers between devices with their start and end apart: 2 -> 2, of which waited for: 1 -> 2; matrix products, arithmetic and copies ran while one was open for 9% -> 2% of each run, Pallas kernels for 0% -> 0%
where the time goes in v1:
time: 62.7 us; the launch traced here: 62.2 us
  waiting for transfers between devices  18.5 us (30%)
  Pallas kernels  15.5 us (25%)
  starting transfers between devices  10.6 us (17%)
  blocking collectives  8.11 us (13%)
  local copies, waits for them, and re-layouts  5.96 us (10%)
  other arithmetic  2.14 us (3%)
  between operations  1.34 us (2%)
    all_to_all x1, waiting for transfers between devices, body(): lax.all_to_all(jnp.broadcast_to(mine[None], (groups,) + mine.shape), 'kgr...  14 us
    pallas_call x1, Pallas kernels, body(): pl.pallas_call(functools.partial(main_kernel, (slots, nval, ncon, nexc)),...  13.8 us
    all_gather x1, blocking collectives, body(): gathered = lax.all_gather(selected, 'scr', axis=0, tiled=False)  8.11 us
    all_to_all x1, starting transfers between devices, body(): lax.all_to_all(jnp.broadcast_to(mine[None], (groups,) + mine.shape), 'kgr...  7.28 us
    all_to_all x1, waiting for transfers between devices, body(): taken = lax.all_to_all(sent, 'scr', 0, 0, tiled=True)  4.56 us
    all_to_all x1, starting transfers between devices, body(): taken = lax.all_to_all(sent, 'scr', 0, 0, tiled=True)  3.32 us
    unnamed x9, local copies, waits for them, and re-layouts  3.25 us
    pallas_call x1, Pallas kernels, body(): pl.pallas_call(functools.partial(pick_kernel, keep), out_shape=jax.ShapeD...  1.74 us
  transfers between devices with their start and end apart: 2, of which 2 were waited for; matrix products, arithmetic and copies ran while one was open for 2% of the time, Pallas kernels for 0%

profile of v1, /device:TPU:0, one launch (start us, length us, event | category | flops | bytes accessed | tf_op | source)
XLA Modules:
  0.0 62.2 jit_solution(17372919887124587483)
XLA Ops:
  0.6 0.0 copy-start.2
  0.6 0.9 %fusion.1 = (bf16[8,256]{1,0:T(8,128)(2,1)S(1)}, bf16[8,256]{1,0:T(8,128)(2,1)S(1)}) fusion(bf16[16,256]{1,0:T(8,128)(2,1)} %bitcast.29), kind=kLoop, calls=%fused_computation.6 | loop fusion | bytes 16384 | tf_op jit(solution)/shard_map/slice | solution.py:125
  1.5 0.8 %pad_maximum_fusion = bf16[72,512]{1,0:T(8,128)(2,1)S(1)} fusion(bf16[32,512]{1,0:T(8,128)(2,1)} %bitcast.27, bf16[8,256]{1,0:T(8,128)(2,1)S(1)} %get-tuple-element.11, bf16[8,256]{1,0:T(8,128)(2,1)S(1)} %get-tuple-element.10, bf16[32,512]{1,0:T(8,128)(2,1)} %bitcast.28), kind=kLoop, calls=%fused_computation.1 | loop fusion | flops 294912 | bytes 147456 | tf_op jit(solution)/shard_map/concatenate | solution.py:127
  2.3 0.8 %broadcast_in_dim.2 = bf16[8,72,512]{2,1,0:T(8,128)(2,1)} broadcast(bf16[72,512]{1,0:T(8,128)(2,1)S(1)} %pad_maximum_fusion), dimensions={1,2} | broadcast | bytes 663552 | tf_op jit(solution)/shard_map/broadcast_in_dim | solution.py:129
  3.1 7.3 %all-to-all-start = ((bf16[8,72,512]{2,1,0:T(8,128)(2,1)}), bf16[8,72,512]{2,1,0:T(8,128)(2,1)S(1)}, u32[]{:S(2)}, u32[]{:S(2)}) async-start(bf16[8,72,512]{2,1,0:T(8,128)(2,1)} %broadcast_in_dim.2), calls=%async_computation | async-start | bytes 1179648 | tf_op jit(solution)/shard_map/all_to_all | solution.py:128
  11.1 1.3 %pad_add_fusion.roles_ref = s32[4]{0:T(128)} fusion(s32[2]{0:T(128)} %bitcast.30, s32[2]{0:T(128)} %bitcast.31), kind=kLoop, calls=%fused_computation.4 | loop fusion | flops 4 | bytes 32 | tf_op jit(solution)/shard_map/concatenate | solution.py:120
  12.3 14.0 %all-to-all-done.all_ref = bf16[8,72,512]{2,1,0:T(8,128)(2,1)S(1)} async-done(((bf16[8,72,512]{2,1,0:T(8,128)(2,1)}), bf16[8,72,512]{2,1,0:T(8,128)(2,1)S(1)}, u32[]{:S(2)}, u32[]{:S(2)}) %all-to-all-start) | async-done | bytes 589856 | tf_op jit(solution)/shard_map/all_to_all | solution.py:128
  26.3 0.0 copy-start
  26.3 0.8 %copy-done = bf16[8,72,512]{2,1,0:T(8,128)(2,1)} copy-done((bf16[8,72,512]{2,1,0:T(8,128)(2,1)}, bf16[8,72,512]{2,1,0:T(8,128)(2,1)S(1)}, u32[]{:S(2)}) %copy-start) | copy-done | bytes 589848
  27.1 1.7 %shard_map.86 = bf16[4,40,512]{2,1,0:T(8,128)(2,1)} custom-call(s32[4]{0:T(128)} %pad_add_fusion.roles_ref, bf16[8,72,512]{2,1,0:T(8,128)(2,1)} %copy-done), custom_call_target="tpu_custom_call" | custom-call | tf_op jit(solution)/shard_map/pallas_call | solution.py:134
  28.8 8.1 %all-gather = bf16[16,40,512]{2,1,0:T(8,128)(2,1)S(1)} all-gather(bf16[4,40,512]{2,1,0:T(8,128)(2,1)} %shard_map.86), channel_id=2, replica_groups=mesh['kgrp'=8,'scr'=4] {'scr'}, dimensions={0}, use_global_device_ids=true | all-gather | bytes 819200 | tf_op jit(solution)/shard_map/all_gather | solution.py:140
  37.0 0.0 copy-done.2
  37.0 0.0 copy-start.1
  37.0 1.1 %copy-done.1 = bf16[8,72,512]{2,1,0:T(8,128)(2,1)S(1)} copy-done((bf16[8,72,512]{2,1,0:T(8,128)(2,1)S(1)}, bf16[8,72,512]{2,1,0:T(8,128)(2,1)}, u32[]{:S(2)}) %copy-start.1) | copy-done | bytes 589848
  38.0 0.0 copy-start.3
  38.0 0.7 %copy-done.3 = s32[4]{0:T(128)S(1)} copy-done((s32[4]{0:T(128)S(1)}, s32[4]{0:T(128)}, u32[]{:S(2)}) %copy-start.3) | copy-done | bytes 40
  38.7 13.8 %shard_map.87 = bf16[4,2,2,32,128]{4,3,2,1,0:T(8,128)(2,1)} custom-call(s32[4]{0:T(128)S(1)} %copy-done.3, bf16[4,4,40,512]{3,2,1,0:T(8,128)(2,1)S(1)} %bitcast.22, bf16[8,72,512]{2,1,0:T(8,128)(2,1)S(1)} %copy-done.1, bf16[2048,512]{1,0:T(8,128)(2,1)S(1)} %bitcast.23), custom_call_target="tpu_custom_call" | custom-call | tf_op jit(solution)/shard_map/pallas_call | solution.py:145
  52.5 3.3 %all-to-all-start.1 = ((bf16[4,2,2,32,128]{4,3,2,1,0:T(8,128)(2,1)}), bf16[4,2,2,32,128]{4,3,2,1,0:T(8,128)(2,1)S(1)}, u32[]{:S(2)}, u32[]{:S(2)}) async-start(bf16[4,2,2,32,128]{4,3,2,1,0:T(8,128)(2,1)} %shard_map.87), calls=%async_computation.1 | async-start | bytes 262144 | tf_op jit(solution)/shard_map/all_to_all | solution.py:168
  55.8 4.6 %all-to-all-done.1 = bf16[4,2,2,32,128]{4,3,2,1,0:T(8,128)(2,1)S(1)} async-done(((bf16[4,2,2,32,128]{4,3,2,1,0:T(8,128)(2,1)}), bf16[4,2,2,32,128]{4,3,2,1,0:T(8,128)(2,1)S(1)}, u32[]{:S(2)}, u32[]{:S(2)}) %all-to-all-start.1) | async-done | bytes 131104 | tf_op jit(solution)/shard_map/all_to_all | solution.py:168
  60.4 0.1 broadcast_multiply_fusion
  60.5 0.1 reshape_squeeze.7
  60.6 0.7 %copy.19 = f32[1,2,256,16]{2,3,1,0:T(8,128)} copy(f32[1,2,256,16]{3,2,1,0:T(8,128)S(1)} %bitcast.25) | data formatting | bytes 65536
  61.3 0.1 copy.16
  61.5 0.7 %reshape.17 = f32[1,2,256,16]{2,3,1,0:T(8,128)} reshape(f32[2,8,32,16]{2,1,3,0:T(8,128)S(1)} %copy.17) | data formatting | bytes 65536 | tf_op jit(solution)/shard_map/reshape | solution.py:176
  (5 shorter events, 0.1 us)
Async XLA Ops:
  0.6 36.3 %copy-start.2 = (bf16[1,2048,512]{2,1,0:T(8,128)(2,1)S(1)}, bf16[1,2048,512]{2,1,0:T(8,128)(2,1)}, u32[]{:S(2)}) copy-start(bf16[1,2048,512]{2,1,0:T(8,128)(2,1)} %param.10) | copy-start | bytes 6291460
  3.1 23.2 %all-to-all-start = ((bf16[8,72,512]{2,1,0:T(8,128)(2,1)}), bf16[8,72,512]{2,1,0:T(8,128)(2,1)S(1)}, u32[]{:S(2)}, u32[]{:S(2)}) async-start(bf16[8,72,512]{2,1,0:T(8,128)(2,1)} %broadcast_in_dim.2), calls=%async_computation | async-start | bytes 1179648 | tf_op jit(solution)/shard_map/all_to_all | solution.py:128
  26.3 0.8 %copy-start = (bf16[8,72,512]{2,1,0:T(8,128)(2,1)}, bf16[8,72,512]{2,1,0:T(8,128)(2,1)S(1)}, u32[]{:S(2)}) copy-start(bf16[8,72,512]{2,1,0:T(8,128)(2,1)S(1)} %all-to-all-done.all_ref) | copy-start | bytes 1769476
  37.0 1.1 %copy-start.1 = (bf16[8,72,512]{2,1,0:T(8,128)(2,1)S(1)}, bf16[8,72,512]{2,1,0:T(8,128)(2,1)}, u32[]{:S(2)}) copy-start(bf16[8,72,512]{2,1,0:T(8,128)(2,1)} %copy-done) | copy-start | bytes 1769476
  38.0 0.7 %copy-start.3 = (s32[4]{0:T(128)S(1)}, s32[4]{0:T(128)}, u32[]{:S(2)}) copy-start(s32[4]{0:T(128)} %pad_add_fusion.roles_ref) | copy-start | bytes 52
  52.5 7.9 %all-to-all-start.1 = ((bf16[4,2,2,32,128]{4,3,2,1,0:T(8,128)(2,1)}), bf16[4,2,2,32,128]{4,3,2,1,0:T(8,128)(2,1)S(1)}, u32[]{:S(2)}, u32[]{:S(2)}) async-start(bf16[4,2,2,32,128]{4,3,2,1,0:T(8,128)(2,1)} %shard_map.87), calls=%async_computation.1 | async-start | bytes 262144 | tf_op jit(solution)/shard_map/all_to_all | solution.py:168

commit v2 on v1

v2 whole, which is shorter than its diff:
```python
import functools

import jax
import jax.numpy as jnp
from jax import lax
from jax.experimental import pallas as pl
from jax.experimental.pallas import tpu as pltpu
from jax.sharding import PartitionSpec as P

LANES = 128
F32 = jnp.float32
BF16 = jnp.bfloat16


def prepare_kernel(con_ref, exc_ref, val_ref, first_ref, second_ref):
    ncon = con_ref.shape[1]
    rows_dev = exc_ref.shape[1]
    step = con_ref.shape[2] // rows_dev
    exc_rows = exc_ref.shape[0] // step
    packed = jnp.concatenate(
        [exc_ref[i * exc_rows : (i + 1) * exc_rows, :] for i in range(step)], axis=1
    )
    for k in range(first_ref.shape[0]):
        first_ref[k, :ncon, :] = con_ref[0]
        first_ref[k, ncon:, :] = packed
        second_ref[k] = val_ref[0]


def pick_kernel(a_ref, b_ref, all_ref, out_ref):
    slots = a_ref.shape[1]
    for p in range(slots):
        out_ref[p] = all_ref[a_ref[0, p]]
        out_ref[slots + p] = all_ref[b_ref[0, p]]


def nt(a, b):
    return lax.dot_general(a, b, (((1,), (1,)), ((), ())), preferred_element_type=F32)


def pair_products(outer, inner, out_ref, column):
    width = inner.shape[1]
    count = inner.shape[0]
    for i in range(outer.shape[0]):
        out_ref[i * count : (i + 1) * count, column : column + width] = (
            outer[i : i + 1, :] * inner
        ).astype(BF16)


def spread_blocks(kernel, out_ref, group):
    block = kernel.shape[0] // group
    tile = out_ref.shape[1] // group
    for i in range(group):
        for q in range(kernel.shape[1] // tile):
            out_ref[q * block : (q + 1) * block, i * tile : (i + 1) * tile] = kernel[
                i * block : (i + 1) * block, q * tile : (q + 1) * tile
            ]


def lay_out(total, parts, nexc):
    flip = total.T
    inner = total.shape[0] // parts
    rows = []
    for s in range(parts):
        rows.append(
            jnp.concatenate(
                [
                    flip[i * nexc : (i + 1) * nexc, s * inner : (s + 1) * inner]
                    for i in range(total.shape[1] // nexc)
                ],
                axis=1,
            )
        )
    return jnp.concatenate(rows, axis=0)


def main_kernel(
    sizes, a_ref, b_ref, me_ref, gath_ref, all_ref, weights_ref, *rest
):
    *out_refs, done_ref, rho_ref, vals_ref, screened_ref, spread_ref, vec_ref, diag_ref = rest
    slots, nval, ncon, nexc = sizes
    shards = gath_ref.shape[0]
    mu_dev = weights_ref.shape[1]
    rows_dev = nval * ncon // shards
    per = LANES // nexc
    parts = done_ref.shape[0]
    lane = lax.broadcasted_iota(jnp.int32, (per * nval, LANES), 1)
    row = lax.broadcasted_iota(jnp.int32, (per * nval, LANES), 0)
    mask = (row // nval == lane // nexc).astype(BF16)
    e_row = lax.broadcasted_iota(jnp.int32, (nexc, LANES), 0)
    e_lane = lax.broadcasted_iota(jnp.int32, (nexc, LANES), 1)
    repeat = (e_lane % nexc == e_row).astype(BF16)
    wide = ncon * per
    src = lax.broadcasted_iota(jnp.int32, (wide, wide), 0)
    dst = lax.broadcasted_iota(jnp.int32, (wide, wide), 1)
    few = nval // parts
    outer = ncon // per
    moved = (src % few) * ncon + (src // few) % outer * per + src // (few * outer)
    order = (moved == dst).astype(BF16)
    for p in range(slots):
        for s in range(shards):
            pair_products(
                gath_ref[s, slots + p, :ncon, :].astype(F32),
                gath_ref[s, p, :ncon, :].astype(F32),
                rho_ref, s * mu_dev,
            )
        screened_ref[...] = jnp.dot(
            rho_ref[...], weights_ref[...], preferred_element_type=F32
        ).astype(BF16)
        pair_products(
            all_ref[a_ref[0, p]].astype(F32), all_ref[b_ref[0, p]].astype(F32), vals_ref, 0
        )
        for way in range(2):
            who = slots + p if way == 0 else p
            for s in range(shards):
                part = gath_ref[s, who, ncon:, :]
                flip = jnp.concatenate(
                    [part[:, i * rows_dev : (i + 1) * rows_dev] for i in range(mu_dev // rows_dev)], axis=0
                )
                vec_ref[s * rows_dev : (s + 1) * rows_dev, :] = lax.dot_general(
                    flip, repeat, (((0,), (0,)), ((), ())), preferred_element_type=F32
                )
            if way == 0:
                kernel = nt(screened_ref[...], vals_ref[...]).astype(BF16)
                count, length = ncon, nval
            else:
                kernel = nt(vals_ref[...], screened_ref[...]).astype(BF16)
                count, length = nval, ncon
            spread_blocks(kernel, spread_ref, count)
            for i in range(count):
                if way == 0:
                    vec = vec_ref[pl.ds(i, length, stride=count), :]
                else:
                    vec = vec_ref[i * length : (i + 1) * length, :]
                vec = vec.astype(BF16)
                tile = per * length
                diag_ref[i * tile : (i + 1) * tile, :] = (
                    jnp.concatenate([vec] * per, axis=0) * mask
                )
            total = jnp.dot(spread_ref[...], diag_ref[...], preferred_element_type=F32)
            if way == 0:
                done = lay_out(total, parts, nexc)
            else:
                total = total.reshape(outer, parts, few, LANES)
                total = jnp.concatenate(
                    [total[q, s] for s in range(parts) for q in range(outer)], axis=0
                )
                done = jnp.dot(
                    lay_out(total, parts, nexc).astype(BF16), order, preferred_element_type=F32
                )
            done = done.astype(BF16)
            for s in range(parts):
                done_ref[s, p, way] = done[s * nexc : (s + 1) * nexc, :]
    for m, out_ref in enumerate(out_refs):
        out_ref[...] = done_ref[m ^ me_ref[0]]


def body(wave_val, wave_con, excite, screening, pair_count, pair_kpoint, pair_partner):
    groups = lax.axis_size("kgrp")
    shards = lax.axis_size("scr")
    slots = pair_kpoint.shape[1]
    nval, mu_dev = wave_val.shape[1:]
    ncon = wave_con.shape[1]
    rows_dev, nexc = excite.shape[1:]
    keep = ncon + nexc * rows_dev // mu_dev
    npb = nval * ncon
    per = LANES // nexc
    parts = nval // per
    split = shards // parts
    vmem = pl.BlockSpec(memory_space=pltpu.VMEM)
    smem = pl.BlockSpec(memory_space=pltpu.SMEM)
    mine_con, mine_val = pl.pallas_call(
        prepare_kernel,
        out_shape=(
            jax.ShapeDtypeStruct((groups, keep, mu_dev), BF16),
            jax.ShapeDtypeStruct((groups, nval, mu_dev), BF16),
        ),
        in_specs=[vmem] * 3,
        out_specs=(vmem, vmem),
    )(wave_con, excite[0].T, wave_val)
    all_con = lax.all_to_all(mine_con, "kgrp", 0, 0, tiled=True)
    all_val = lax.all_to_all(mine_val, "kgrp", 0, 0, tiled=True)
    selected = pl.pallas_call(
        pick_kernel,
        out_shape=jax.ShapeDtypeStruct((2 * slots, keep, mu_dev), BF16),
        in_specs=[smem, smem, vmem],
        out_specs=vmem,
    )(pair_kpoint, pair_partner, all_con)
    gathered = lax.all_gather(selected, "scr", axis=0, tiled=False)
    direct = split == 1 and shards & (shards - 1) == 0
    me = lax.axis_index("scr") if direct else 0
    block = jax.ShapeDtypeStruct((slots, 2, nexc, per * ncon), BF16)
    partial = pl.pallas_call(
        functools.partial(main_kernel, (slots, nval, ncon, nexc)),
        out_shape=(block,) * parts,
        in_specs=[smem, smem, smem, vmem, vmem, vmem],
        out_specs=(vmem,) * parts,
        scratch_shapes=[
            pltpu.VMEM((parts,) + block.shape, BF16),
            pltpu.VMEM((npb, shards * mu_dev), BF16),
            pltpu.VMEM((npb, mu_dev), BF16),
            pltpu.VMEM((npb, mu_dev), BF16),
            pltpu.VMEM((npb // per, npb * per), BF16),
            pltpu.VMEM((npb, LANES), F32),
            pltpu.VMEM((npb * per, LANES), BF16),
        ],
        compiler_params=pltpu.CompilerParams(vmem_limit_bytes=48 * 2**20),
    )(
        pair_kpoint, pair_partner, jnp.full((1,), me, jnp.int32),
        gathered, all_val, screening[0],
    )
    if direct:
        taken = [partial[0]] + [
            lax.ppermute(partial[m], "scr", [(i, i ^ m) for i in range(shards)])
            for m in range(shards - 1, 0, -1)
        ]
    else:
        sent = jnp.stack(partial).reshape(parts, slots, 2, nexc, split, rows_dev)
        sent = sent.transpose(0, 4, 1, 2, 3, 5).reshape(shards, slots, 2, nexc, rows_dev)
        sent = lax.all_to_all(sent, "scr", 0, 0, tiled=True)
        taken = [sent[i] for i in range(shards)]
    live = (jnp.arange(slots, dtype=jnp.int32) < pair_count[0]).astype(F32)
    summed = sum(t.astype(F32) for t in taken) * live[:, None, None, None]
    return (
        summed[None, :, 0].transpose(0, 1, 3, 2),
        summed[None, :, 1].transpose(0, 1, 3, 2),
    )


def solution(mesh):
    return jax.shard_map(
        body,
        mesh=mesh,
        in_specs=(
            P("kgrp", None, "scr"),
            P("kgrp", None, "scr"),
            P("kgrp", "scr", None),
            P("kgrp", None, "scr"),
            P("kgrp"),
            P("kgrp", None),
            P("kgrp", None),
        ),
        out_specs=(P("kgrp", None, "scr", None), P("kgrp", None, "scr", None)),
        check_vma=False,
    )
```

time: 62.7 us -> 53.8 us (0.86)
  blocking collectives: 8.11 us -> 26.4 us
  waiting for transfers between devices: 18.5 us -> 2.42 us
  local copies, waits for them, and re-layouts: 5.96 us -> 0.65 us
  starting transfers between devices: 10.6 us -> 5.45 us
  other arithmetic: 2.14 us -> 0.08 us
  Pallas kernels: 15.5 us -> 17 us
    all_to_all x2 -> x1, waiting for transfers between devices: 18.5 us -> 0.01 us  [body(): all_val = lax.all_to_all(mine_val, 'kgrp', 0, 0, tiled=True)]
    all_to_all x0 -> x1, blocking collectives: none -> 18.3 us  [body(): all_con = lax.all_to_all(mine_con, 'kgrp', 0, 0, tiled=True)]
    all_to_all x2 -> x1, starting transfers between devices: 10.6 us -> 3.41 us  [body(): all_val = lax.all_to_all(mine_val, 'kgrp', 0, 0, tiled=True)]
    unnamed x9 -> x6, local copies, waits for them, and re-layouts: 3.25 us -> 0.02 us
    ppermute x0 -> x3, waiting for transfers between devices: none -> 2.42 us  [body(): lax.ppermute(partial[m], 'scr', [(i, i ^ m) for i in range(shards)])]
    concatenate x2 -> x0, other arithmetic: 2.04 us -> none  [the longest x1 1.26 us: body(): roles = jnp.concatenate([pair_kpoint[0], pair_partner[0]])]
    ppermute x0 -> x3, starting transfers between devices: none -> 2.04 us  [body(): lax.ppermute(partial[m], 'scr', [(i, i ^ m) for i in range(shards)])]
    pallas_call x1 -> x2, Pallas kernels: 1.74 us -> 3.42 us  [the longest x1 1.77 us: body(): pl.pallas_call(prepare_kernel, out_shape=(jax.ShapeDtypeStruct((groups, k...]
  transfers between devices with their start and end apart: 2 -> 4, of which waited for: 2 -> 2; matrix products, arithmetic and copies ran while one was open for 2% -> 0% of each run, Pallas kernels for 0% -> 3%
where the time goes in v2:
time: 53.8 us; the launch traced here: 53.4 us
  blocking collectives  26.4 us (49%)
  Pallas kernels  17 us (32%)
  starting transfers between devices  5.45 us (10%)
  waiting for transfers between devices  2.42 us (4%)
  between operations  1.34 us (2%)
  local copies, waits for them, and re-layouts  0.65 us (1%)
    all_to_all x1, blocking collectives, body(): all_con = lax.all_to_all(mine_con, 'kgrp', 0, 0, tiled=True)  18.3 us
    pallas_call x1, Pallas kernels, body(): pl.pallas_call(functools.partial(main_kernel, (slots, nval, ncon, nexc)),...  13.6 us
    all_gather x1, blocking collectives, body(): gathered = lax.all_gather(selected, 'scr', axis=0, tiled=False)  8.11 us
    all_to_all x1, starting transfers between devices, body(): all_val = lax.all_to_all(mine_val, 'kgrp', 0, 0, tiled=True)  3.41 us
    ppermute x3, waiting for transfers between devices, body(): lax.ppermute(partial[m], 'scr', [(i, i ^ m) for i in range(shards)])  2.42 us
    ppermute x3, starting transfers between devices, body(): lax.ppermute(partial[m], 'scr', [(i, i ^ m) for i in range(shards)])  2.04 us
    pallas_call x1, Pallas kernels, body(): pl.pallas_call(prepare_kernel, out_shape=(jax.ShapeDtypeStruct((groups, k...  1.77 us
    pallas_call x1, Pallas kernels, body(): pl.pallas_call(pick_kernel, out_shape=jax.ShapeDtypeStruct((2 * slots, ke...  1.66 us
  transfers between devices with their start and end apart: 4, of which 2 were waited for; matrix products, arithmetic and copies ran while one was open for 0% of the time, Pallas kernels for 3%

profile of v2, /device:TPU:0, one launch (start us, length us, event | category | flops | bytes accessed | tf_op | source)
XLA Modules:
  0.0 53.4 jit_solution(6874082532703130906)
XLA Ops:
  0.6 0.0 copy-start.2
  0.6 0.0 copy-start.1
  0.7 0.0 copy-start
  0.7 1.8 %shard_map.86 = (bf16[8,40,512]{2,1,0:T(8,128)(2,1)}, bf16[8,32,512]{2,1,0:T(8,128)(2,1)}) custom-call(bf16[1,32,512]{2,1,0:T(8,128)(2,1)} %con_ref.1, bf16[16,256]{1,0:T(8,128)(2,1)} %bitcast.18, bf16[1,32,512]{2,1,0:T(8,128)(2,1)} %val_ref.1), custom_call_target="tpu_custom_call" | custom-call | tf_op jit(solution)/shard_map/pallas_call | solution.py:171
  2.4 18.3 %all_to_all.10.all_ref = bf16[8,40,512]{2,1,0:T(8,128)(2,1)} all-to-all(bf16[8,40,512]{2,1,0:T(8,128)(2,1)} %get-tuple-element.8), channel_id=1, replica_groups=mesh['kgrp'=8,'scr'=4] {'kgrp'}, dimensions={0} | all-to-all | bytes 655360 | tf_op jit(solution)/shard_map/all_to_all | solution.py:180
  20.7 3.4 %all-to-all-start.1 = ((bf16[8,32,512]{2,1,0:T(8,128)(2,1)}), bf16[8,32,512]{2,1,0:T(8,128)(2,1)S(1)}, u32[]{:S(2)}, u32[]{:S(2)}) async-start(bf16[8,32,512]{2,1,0:T(8,128)(2,1)} %get-tuple-element.9), calls=%async_computation.1 | async-start | bytes 524288 | tf_op jit(solution)/shard_map/all_to_all | solution.py:181
  24.8 1.7 %shard_map.87 = bf16[4,40,512]{2,1,0:T(8,128)(2,1)} custom-call(s32[1,2]{1,0:T(1,128)} %a_ref.3, s32[1,2]{1,0:T(1,128)} %b_ref.3, bf16[8,40,512]{2,1,0:T(8,128)(2,1)} %all_to_all.10.all_ref), custom_call_target="tpu_custom_call" | custom-call | tf_op jit(solution)/shard_map/pallas_call | solution.py:182
  26.5 8.1 %all-gather = bf16[16,40,512]{2,1,0:T(8,128)(2,1)S(1)} all-gather(bf16[4,40,512]{2,1,0:T(8,128)(2,1)} %shard_map.87), channel_id=2, replica_groups=mesh['kgrp'=8,'scr'=4] {'scr'}, dimensions={0}, use_global_device_ids=true | all-gather | bytes 819200 | tf_op jit(solution)/shard_map/all_gather | solution.py:188
  34.6 0.0 all-to-all-done.1.all_ref
  34.6 0.0 copy-done.2
  34.6 0.0 copy-done.1
  34.6 0.0 copy-done
  34.6 13.6 %shard_map.88 = (bf16[2,2,16,256]{3,2,1,0:T(8,128)(2,1)S(1)}, bf16[2,2,16,256]{3,2,1,0:T(8,128)(2,1)S(1)}, bf16[2,2,16,256]{3,2,1,0:T(8,128)(2,1)S(1)}, bf16[2,2,16,256]{3,2,1,0:T(8,128)(2,1)S(1)}) custom-call(s32[1,2]{1,0:T(1,128)S(1)} %copy-done.1, s32[1,2]{1,0:T(1,128)S(1)} %copy-done.2, s32[1]{0:T(128)} %bitcast.me_ref, ...), custom_call_target="tpu_custom_call" | custom-call | tf_op jit(solution)/shard_map/pallas_call | solution.py:192
  48.2 0.5 collective-permute-start
  48.7 1.5 %collective-permute-start.1 = (bf16[2,2,16,256]{3,2,1,0:T(8,128)(2,1)S(1)}, bf16[2,2,16,256]{3,2,1,0:T(8,128)(2,1)S(1)}, u32[]{:S(2)}, u32[]{:S(2)}) collective-permute-start(bf16[2,2,16,256]{3,2,1,0:T(8,128)(2,1)S(1)} %get-tuple-element.12), channel_id=1, source_target_pairs={{0,2},{1,3},{2,0},{3,1},{4,6},{5,7},{6,4},{7,5},{8,10},{9,11},{10,... | collective-permute-start | bytes 98312 | tf_op jit(solution)/shard_map/ppermute | solution.py:213
  50.2 0.0 collective-permute-start.2
  50.3 1.4 %collective-permute-done = bf16[2,2,16,256]{3,2,1,0:T(8,128)(2,1)S(1)} collective-permute-done((bf16[2,2,16,256]{3,2,1,0:T(8,128)(2,1)S(1)}, bf16[2,2,16,256]{3,2,1,0:T(8,128)(2,1)S(1)}, u32[]{:S(2)}, u32[]{:S(2)}) %collective-permute-start) | collective-permute-done | bytes 32800 | tf_op jit(solution)/shard_map/ppermute | solution.py:213
  51.6 1.1 %collective-permute-done.1 = bf16[2,2,16,256]{3,2,1,0:T(8,128)(2,1)S(1)} collective-permute-done((bf16[2,2,16,256]{3,2,1,0:T(8,128)(2,1)S(1)}, bf16[2,2,16,256]{3,2,1,0:T(8,128)(2,1)S(1)}, u32[]{:S(2)}, u32[]{:S(2)}) %collective-permute-start.1) | collective-permute-done | bytes 32800 | tf_op jit(solution)/shard_map/ppermute | solution.py:213
  52.7 0.0 collective-permute-done.2
  52.7 0.1 add_multiply_fusion
  52.7 0.6 %slice_bitcast_fusion = (f32[1,2,256,16]{2,3,1,0:T(8,128)}, f32[1,2,256,16]{2,3,1,0:T(8,128)}) fusion(f32[2,2,16,256]{3,2,1,0:T(8,128)S(1)} %add_multiply_fusion), kind=kLoop, calls=%fused_computation.1 | loop fusion | bytes 131072 | tf_op jit(solution)/shard_map/transpose | solution.py:225
  (1 shorter events, 0.0 us)
Async XLA Ops:
  0.6 33.9 %copy-start.2 = (s32[1,2]{1,0:T(1,128)S(1)}, s32[1,2]{1,0:T(1,128)}, u32[]{:S(2)}) copy-start(s32[1,2]{1,0:T(1,128)} %b_ref.3) | copy-start | bytes 28
  0.6 33.9 %copy-start.1 = (s32[1,2]{1,0:T(1,128)S(1)}, s32[1,2]{1,0:T(1,128)}, u32[]{:S(2)}) copy-start(s32[1,2]{1,0:T(1,128)} %a_ref.3) | copy-start | bytes 28
  0.7 33.9 %copy-start = (bf16[1,2048,512]{2,1,0:T(8,128)(2,1)S(1)}, bf16[1,2048,512]{2,1,0:T(8,128)(2,1)}, u32[]{:S(2)}) copy-start(bf16[1,2048,512]{2,1,0:T(8,128)(2,1)} %param.10) | copy-start | bytes 6291460
  20.7 13.8 %all-to-all-start.1 = ((bf16[8,32,512]{2,1,0:T(8,128)(2,1)}), bf16[8,32,512]{2,1,0:T(8,128)(2,1)S(1)}, u32[]{:S(2)}, u32[]{:S(2)}) async-start(bf16[8,32,512]{2,1,0:T(8,128)(2,1)} %get-tuple-element.9), calls=%async_computation.1 | async-start | bytes 524288 | tf_op jit(solution)/shard_map/all_to_all | solution.py:181
  48.2 3.4 %collective-permute-start = (bf16[2,2,16,256]{3,2,1,0:T(8,128)(2,1)S(1)}, bf16[2,2,16,256]{3,2,1,0:T(8,128)(2,1)S(1)}, u32[]{:S(2)}, u32[]{:S(2)}) collective-permute-start(bf16[2,2,16,256]{3,2,1,0:T(8,128)(2,1)S(1)} %get-tuple-element.11), channel_id=1, source_target_pairs={{0,3},{1,2},{2,1},{3,0},{4,7},{5,6},{6,5},{7,4},{8,11},{9,10},{10,... | collective-permute-start | bytes 98312 | tf_op jit(solution)/shard_map/ppermute | solution.py:213
  48.7 3.9 %collective-permute-start.1 = (bf16[2,2,16,256]{3,2,1,0:T(8,128)(2,1)S(1)}, bf16[2,2,16,256]{3,2,1,0:T(8,128)(2,1)S(1)}, u32[]{:S(2)}, u32[]{:S(2)}) collective-permute-start(bf16[2,2,16,256]{3,2,1,0:T(8,128)(2,1)S(1)} %get-tuple-element.12), channel_id=1, source_target_pairs={{0,2},{1,3},{2,0},{3,1},{4,6},{5,7},{6,4},{7,5},{8,10},{9,11},{10,... | collective-permute-start | bytes 98312 | tf_op jit(solution)/shard_map/ppermute | solution.py:213
  50.2 2.4 %collective-permute-start.2 = (bf16[2,2,16,256]{3,2,1,0:T(8,128)(2,1)S(1)}, bf16[2,2,16,256]{3,2,1,0:T(8,128)(2,1)S(1)}, u32[]{:S(2)}, u32[]{:S(2)}) collective-permute-start(bf16[2,2,16,256]{3,2,1,0:T(8,128)(2,1)S(1)} %get-tuple-element.13), channel_id=1, source_target_pairs={{0,1},{1,0},{2,3},{3,2},{4,5},{5,4},{6,7},{7,6},{8,9},{9,8},{10,11... | collective-permute-start | bytes 98312 | tf_op jit(solution)/shard_map/ppermute | solution.py:213

commit v3 on v2

--- a/solution.py
+++ b/solution.py
@@ -41,7 +41,7 @@
     width = inner.shape[1]
     count = inner.shape[0]
     for i in range(outer.shape[0]):
-        out_ref[i * count : (i + 1) * count, column : column + width] = (
+        out_ref[i * count : (i + 1) * count, pl.ds(column, width)] = (
             outer[i : i + 1, :] * inner
         ).astype(BF16)
 
@@ -73,13 +73,31 @@
     return jnp.concatenate(rows, axis=0)
 
 
+def screen_kernel(sizes, ids_ref, weights_ref, *rest):
+    slots, ncon, shards = sizes
+    gath_refs, (out_ref, rho_ref) = rest[:shards], rest[shards:]
+    mu_dev = weights_ref.shape[1]
+    for p in range(slots):
+        for m, gath_ref in enumerate(gath_refs):
+            pair_products(
+                gath_ref[slots + p, :ncon, :].astype(F32),
+                gath_ref[p, :ncon, :].astype(F32),
+                rho_ref, pl.multiple_of(ids_ref[m] * mu_dev, mu_dev),
+            )
+        out_ref[p] = jnp.dot(
+            rho_ref[...], weights_ref[...], preferred_element_type=F32
+        ).astype(BF16)
+
+
 def main_kernel(
-    sizes, a_ref, b_ref, me_ref, gath_ref, all_ref, weights_ref, *rest
+    sizes, a_ref, b_ref, ids_ref, all_ref, screened_ref, *rest
 ):
-    *out_refs, done_ref, rho_ref, vals_ref, screened_ref, spread_ref, vec_ref, diag_ref = rest
+    shards, direct = sizes[4:]
+    sizes = sizes[:4]
+    gath_refs, rest = rest[:shards], rest[shards:]
+    *out_refs, done_ref, vals_ref, spread_ref, vec_ref, diag_ref = rest
     slots, nval, ncon, nexc = sizes
-    shards = gath_ref.shape[0]
-    mu_dev = weights_ref.shape[1]
+    mu_dev = screened_ref.shape[2]
     rows_dev = nval * ncon // shards
     per = LANES // nexc
     parts = done_ref.shape[0]
@@ -97,33 +115,25 @@
     moved = (src % few) * ncon + (src // few) % outer * per + src // (few * outer)
     order = (moved == dst).astype(BF16)
     for p in range(slots):
-        for s in range(shards):
-            pair_products(
-                gath_ref[s, slots + p, :ncon, :].astype(F32),
-                gath_ref[s, p, :ncon, :].astype(F32),
-                rho_ref, s * mu_dev,
-            )
-        screened_ref[...] = jnp.dot(
-            rho_ref[...], weights_ref[...], preferred_element_type=F32
-        ).astype(BF16)
         pair_products(
             all_ref[a_ref[0, p]].astype(F32), all_ref[b_ref[0, p]].astype(F32), vals_ref, 0
         )
         for way in range(2):
             who = slots + p if way == 0 else p
-            for s in range(shards):
-                part = gath_ref[s, who, ncon:, :]
+            for gath_ref, m in zip(gath_refs, range(shards)):
+                part = gath_ref[who, ncon:, :]
+                at = pl.multiple_of(ids_ref[m] * rows_dev, rows_dev)
                 flip = jnp.concatenate(
                     [part[:, i * rows_dev : (i + 1) * rows_dev] for i in range(mu_dev // rows_dev)], axis=0
                 )
-                vec_ref[s * rows_dev : (s + 1) * rows_dev, :] = lax.dot_general(
+                vec_ref[pl.ds(at, rows_dev), :] = lax.dot_general(
                     flip, repeat, (((0,), (0,)), ((), ())), preferred_element_type=F32
                 )
             if way == 0:
-                kernel = nt(screened_ref[...], vals_ref[...]).astype(BF16)
+                kernel = nt(screened_ref[p], vals_ref[...]).astype(BF16)
                 count, length = ncon, nval
             else:
-                kernel = nt(vals_ref[...], screened_ref[...]).astype(BF16)
+                kernel = nt(vals_ref[...], screened_ref[p]).astype(BF16)
                 count, length = nval, ncon
             spread_blocks(kernel, spread_ref, count)
             for i in range(count):
@@ -151,7 +161,7 @@
             for s in range(parts):
                 done_ref[s, p, way] = done[s * nexc : (s + 1) * nexc, :]
     for m, out_ref in enumerate(out_refs):
-        out_ref[...] = done_ref[m ^ me_ref[0]]
+        out_ref[...] = done_ref[ids_ref[m] if direct else m]
 
 
 def body(wave_val, wave_con, excite, screening, pair_count, pair_kpoint, pair_partner):
@@ -176,6 +186,7 @@
         ),
         in_specs=[vmem] * 3,
         out_specs=(vmem, vmem),
+        cost_estimate=pl.CostEstimate(flops=0, transcendentals=0, bytes_accessed=6 * 2**20),
     )(wave_con, excite[0].T, wave_val)
     all_con = lax.all_to_all(mine_con, "kgrp", 0, 0, tiled=True)
     all_val = lax.all_to_all(mine_val, "kgrp", 0, 0, tiled=True)
@@ -184,30 +195,48 @@
         out_shape=jax.ShapeDtypeStruct((2 * slots, keep, mu_dev), BF16),
         in_specs=[smem, smem, vmem],
         out_specs=vmem,
+        compiler_params=pltpu.CompilerParams(vmem_limit_bytes=8 * 2**20),
     )(pair_kpoint, pair_partner, all_con)
-    gathered = lax.all_gather(selected, "scr", axis=0, tiled=False)
     direct = split == 1 and shards & (shards - 1) == 0
-    me = lax.axis_index("scr") if direct else 0
+    if direct:
+        ids = lax.axis_index("scr") ^ jnp.arange(shards, dtype=jnp.int32)
+        found = {0: selected}
+        step = shards
+        while step > 1:
+            step //= 2
+            for m in sorted(found):
+                found[m | step] = lax.ppermute(
+                    found[m], "scr", [(i, i ^ step) for i in range(shards)]
+                )
+        gathered = [found[m] for m in range(shards)]
+    else:
+        ids = jnp.arange(shards, dtype=jnp.int32)
+        gathered = lax.all_gather(selected, "scr", axis=0, tiled=False)
+        gathered = [gathered[m] for m in range(shards)]
     block = jax.ShapeDtypeStruct((slots, 2, nexc, per * ncon), BF16)
+    limit = pltpu.CompilerParams(vmem_limit_bytes=24 * 2**20)
+    screened = pl.pallas_call(
+        functools.partial(screen_kernel, (slots, ncon, shards)),
+        out_shape=jax.ShapeDtypeStruct((slots, npb, mu_dev), BF16),
+        in_specs=[smem] + [vmem] * (1 + shards),
+        out_specs=vmem,
+        scratch_shapes=[pltpu.VMEM((npb, shards * mu_dev), BF16)],
+        compiler_params=limit,
+    )(ids, screening[0], *gathered)
     partial = pl.pallas_call(
-        functools.partial(main_kernel, (slots, nval, ncon, nexc)),
+        functools.partial(main_kernel, (slots, nval, ncon, nexc, shards, direct)),
         out_shape=(block,) * parts,
-        in_specs=[smem, smem, smem, vmem, vmem, vmem],
+        in_specs=[smem] * 3 + [vmem] * (2 + shards),
         out_specs=(vmem,) * parts,
         scratch_shapes=[
             pltpu.VMEM((parts,) + block.shape, BF16),
-            pltpu.VMEM((npb, shards * mu_dev), BF16),
-            pltpu.VMEM((npb, mu_dev), BF16),
             pltpu.VMEM((npb, mu_dev), BF16),
             pltpu.VMEM((npb // per, npb * per), BF16),
             pltpu.VMEM((npb, LANES), F32),
             pltpu.VMEM((npb * per, LANES), BF16),
         ],
-        compiler_params=pltpu.CompilerParams(vmem_limit_bytes=48 * 2**20),
-    )(
-        pair_kpoint, pair_partner, jnp.full((1,), me, jnp.int32),
-        gathered, all_val, screening[0],
-    )
+        compiler_params=limit,
+    )(pair_kpoint, pair_partner, ids, all_val, screened, *gathered)
     if direct:
         taken = [partial[0]] + [
             lax.ppermute(partial[m], "scr", [(i, i ^ m) for i in range(shards)])

time: 53.8 us -> 55.8 us (1.037)
  blocking collectives: 26.4 us -> 18.2 us
  waiting for transfers between devices: 2.42 us -> 7.74 us
  local copies, waits for them, and re-layouts: 0.65 us -> 3.54 us
  starting transfers between devices: 5.45 us -> 6.93 us
    all_gather x1 -> x0, blocking collectives: 8.11 us -> none  [body(): gathered = lax.all_gather(selected, 'scr', axis=0, tiled=False)]
    ppermute x0 -> x3, waiting for transfers between devices: none -> 4.52 us  [body(): lax.ppermute(found[m], 'scr', [(i, i ^ step) for i in range(shards)])]
    unnamed x6 -> x10, local copies, waits for them, and re-layouts: 0.02 us -> 2.9 us
    pallas_call x1 -> x2, Pallas kernels: 13.6 us -> 15.4 us  [the longest x1 9.38 us: body(): pl.pallas_call(functools.partial(main_kernel, (slots, nval, ncon, nexc, s...]
    ppermute x0 -> x3, starting transfers between devices: none -> 1.59 us  [body(): lax.ppermute(found[m], 'scr', [(i, i ^ step) for i in range(shards)])]
    pallas_call x1, Pallas kernels: 1.66 us -> 0.56 us  [body(): pl.pallas_call(pick_kernel, out_shape=jax.ShapeDtypeStruct((2 * slots, ke...]
    ppermute x3, waiting for transfers between devices: 2.42 us -> 3.22 us  [body(): lax.ppermute(partial[m], 'scr', [(i, i ^ m) for i in range(shards)])]
  transfers between devices with their start and end apart: 4 -> 7, of which waited for: 2 -> 4; matrix products, arithmetic and copies ran while one was open for 0% -> 0% of each run, Pallas kernels for 3% -> 12%
where the time goes in v3:
time: 55.8 us; the launch traced here: 55.4 us
  blocking collectives  18.2 us (33%)
  Pallas kernels  17.5 us (31%)
  waiting for transfers between devices  7.74 us (14%)
  starting transfers between devices  6.93 us (12%)
  local copies, waits for them, and re-layouts  3.54 us (6%)
  between operations  1.37 us (2%)
    all_to_all x1, blocking collectives, body(): all_con = lax.all_to_all(mine_con, 'kgrp', 0, 0, tiled=True)  18.2 us
    pallas_call x1, Pallas kernels, body(): pl.pallas_call(functools.partial(main_kernel, (slots, nval, ncon, nexc, s...  9.38 us
    pallas_call x1, Pallas kernels, body(): pl.pallas_call(functools.partial(screen_kernel, (slots, ncon, shards)), o...  5.98 us
    ppermute x3, waiting for transfers between devices, body(): lax.ppermute(found[m], 'scr', [(i, i ^ step) for i in range(shards)])  4.52 us
    all_to_all x1, starting transfers between devices, body(): all_val = lax.all_to_all(mine_val, 'kgrp', 0, 0, tiled=True)  3.41 us
    ppermute x3, waiting for transfers between devices, body(): lax.ppermute(partial[m], 'scr', [(i, i ^ m) for i in range(shards)])  3.22 us
    unnamed x10, local copies, waits for them, and re-layouts  2.9 us
    ppermute x3, starting transfers between devices, body(): lax.ppermute(partial[m], 'scr', [(i, i ^ m) for i in range(shards)])  1.93 us
  transfers between devices with their start and end apart: 7, of which 4 were waited for; matrix products, arithmetic and copies ran while one was open for 0% of the time, Pallas kernels for 12%

profile of v3, /device:TPU:0, one launch (start us, length us, event | category | flops | bytes accessed | tf_op | source)
XLA Modules:
  0.0 55.4 jit_solution(8270015548239345231)
XLA Ops:
  0.6 1.6 %shard_map.86 = (bf16[8,40,512]{2,1,0:T(8,128)(2,1)}, bf16[8,32,512]{2,1,0:T(8,128)(2,1)}) custom-call(bf16[1,32,512]{2,1,0:T(8,128)(2,1)} %con_ref.1, bf16[16,256]{1,0:T(8,128)(2,1)} %bitcast.15, bf16[1,32,512]{2,1,0:T(8,128)(2,1)} %val_ref.1), custom_call_target="tpu_custom_call" | custom-call | bytes 6291456 | tf_op jit(solution)/shard_map/pallas_call | solution.py:181
  2.3 18.2 %all_to_all.10.all_ref = bf16[8,40,512]{2,1,0:T(8,128)(2,1)S(1)} all-to-all(bf16[8,40,512]{2,1,0:T(8,128)(2,1)} %get-tuple-element.9), channel_id=1, replica_groups=mesh['kgrp'=8,'scr'=4] {'kgrp'}, dimensions={0} | all-to-all | bytes 655360 | tf_op jit(solution)/shard_map/all_to_all | solution.py:191
  20.4 3.4 %all-to-all-start = ((bf16[8,32,512]{2,1,0:T(8,128)(2,1)}), bf16[8,32,512]{2,1,0:T(8,128)(2,1)S(1)}, u32[]{:S(2)}, u32[]{:S(2)}) async-start(bf16[8,32,512]{2,1,0:T(8,128)(2,1)} %get-tuple-element.8), calls=%async_computation | async-start | bytes 524288 | tf_op jit(solution)/shard_map/all_to_all | solution.py:192
  23.9 0.0 copy-start.1
  23.9 0.6 %copy-done.1 = s32[1,2]{1,0:T(1,128)S(1)} copy-done((s32[1,2]{1,0:T(1,128)S(1)}, s32[1,2]{1,0:T(1,128)}, u32[]{:S(2)}) %copy-start.1) | copy-done | bytes 32
  24.5 0.0 copy-start.3
  24.5 0.7 %copy-done.3 = s32[1,2]{1,0:T(1,128)S(1)} copy-done((s32[1,2]{1,0:T(1,128)S(1)}, s32[1,2]{1,0:T(1,128)}, u32[]{:S(2)}) %copy-start.3) | copy-done | bytes 32
  25.2 0.6 %shard_map.87.rest_0_ = bf16[4,40,512]{2,1,0:T(8,128)(2,1)S(1)} custom-call(s32[1,2]{1,0:T(1,128)S(1)} %copy-done.1, s32[1,2]{1,0:T(1,128)S(1)} %copy-done.3, bf16[8,40,512]{2,1,0:T(8,128)(2,1)S(1)} %all_to_all.10.all_ref), custom_call_target="tpu_custom_call" | custom-call | tf_op jit(solution)/shard_map/pallas_call | solution.py:193
  25.7 1.6 %collective-permute-start.1 = (bf16[4,40,512]{2,1,0:T(8,128)(2,1)S(1)}, bf16[4,40,512]{2,1,0:T(8,128)(2,1)S(1)}, u32[]{:S(2)}, u32[]{:S(2)}) collective-permute-start(bf16[4,40,512]{2,1,0:T(8,128)(2,1)S(1)} %shard_map.87.rest_0_), channel_id=1, source_target_pairs={{0,2},{1,3},{2,0},{3,1},{4,6},{5,7},{6,4},{7,5},{8,10},{9,11},{10,... | collective-permute-start | bytes 491528 | tf_op jit(solution)/shard_map/ppermute | solution.py:208
  27.3 0.0 collective-permute-start
  27.3 3.8 %collective-permute-done.1.rest_2_ = bf16[4,40,512]{2,1,0:T(8,128)(2,1)S(1)} collective-permute-done((bf16[4,40,512]{2,1,0:T(8,128)(2,1)S(1)}, bf16[4,40,512]{2,1,0:T(8,128)(2,1)S(1)}, u32[]{:S(2)}, u32[]{:S(2)}) %collective-permute-start.1) | collective-permute-done | bytes 163872 | tf_op jit(solution)/shard_map/ppermute | solution.py:208
  31.1 0.0 collective-permute-start.2
  31.8 0.0 collective-permute-done.rest_1_
  31.8 0.7 %collective-permute-done.2.rest_3_ = bf16[4,40,512]{2,1,0:T(8,128)(2,1)S(1)} collective-permute-done((bf16[4,40,512]{2,1,0:T(8,128)(2,1)S(1)}, bf16[4,40,512]{2,1,0:T(8,128)(2,1)S(1)}, u32[]{:S(2)}, u32[]{:S(2)}) %collective-permute-start.2) | collective-permute-done | bytes 163872 | tf_op jit(solution)/shard_map/ppermute | solution.py:208
  32.5 0.0 copy-start
  32.5 1.6 %copy-done = bf16[1,2048,512]{2,1,0:T(8,128)(2,1)S(1)} copy-done((bf16[1,2048,512]{2,1,0:T(8,128)(2,1)S(1)}, bf16[1,2048,512]{2,1,0:T(8,128)(2,1)}, u32[]{:S(2)}) %copy-start) | copy-done | bytes 2097176
  34.1 0.0 copy-start.2
  34.1 0.0 copy-start.4
  34.1 6.0 %shard_map.88.screened_ref = bf16[2,1024,512]{2,1,0:T(8,128)(2,1)S(1)} custom-call(s32[4]{0:T(128)S(1)} %iota_xor_fusion.ids_ref, bf16[2048,512]{1,0:T(8,128)(2,1)S(1)} %bitcast.14, bf16[4,40,512]{2,1,0:T(8,128)(2,1)S(1)} %shard_map.87.rest_0_, bf16[4,40,512]{2,1,0:T(8,128)(2,1)S(1)} %collective-permute-done.rest_1_, ...), custom_call_target="tpu_custom_call" | custom-call | tf_op jit(solution)/shard_map/pallas_call | solution.py:218
  40.1 0.0 all-to-all-done.all_ref
  40.1 0.0 copy-done.2
  40.1 0.0 copy-done.4
  40.1 9.4 %shard_map.89 = (bf16[2,2,16,256]{3,2,1,0:T(8,128)(2,1)S(1)}, bf16[2,2,16,256]{3,2,1,0:T(8,128)(2,1)S(1)}, bf16[2,2,16,256]{3,2,1,0:T(8,128)(2,1)S(1)}, bf16[2,2,16,256]{3,2,1,0:T(8,128)(2,1)S(1)}) custom-call(s32[1,2]{1,0:T(1,128)S(1)} %copy-done.2, s32[1,2]{1,0:T(1,128)S(1)} %copy-done.4, s32[4]{0:T(128)S(1)} %iota_xor_fusion.ids_ref, ...), custom_call_target="tpu_custom_call" | custom-call | tf_op jit(solution)/shard_map/pallas_call | solution.py:226
  49.5 0.2 collective-permute-start.5
  49.7 1.5 %collective-permute-start.4 = (bf16[2,2,16,256]{3,2,1,0:T(8,128)(2,1)S(1)}, bf16[2,2,16,256]{3,2,1,0:T(8,128)(2,1)S(1)}, u32[]{:S(2)}, u32[]{:S(2)}) collective-permute-start(bf16[2,2,16,256]{3,2,1,0:T(8,128)(2,1)S(1)} %get-tuple-element.12), channel_id=1, source_target_pairs={{0,2},{1,3},{2,0},{3,1},{4,6},{5,7},{6,4},{7,5},{8,10},{9,11},{10,... | collective-permute-start | bytes 98312 | tf_op jit(solution)/shard_map/ppermute | solution.py:242
  51.3 0.2 collective-permute-start.3
  51.5 0.0 collective-permute-done.5
  51.5 2.2 %collective-permute-done.4 = bf16[2,2,16,256]{3,2,1,0:T(8,128)(2,1)S(1)} collective-permute-done((bf16[2,2,16,256]{3,2,1,0:T(8,128)(2,1)S(1)}, bf16[2,2,16,256]{3,2,1,0:T(8,128)(2,1)S(1)}, u32[]{:S(2)}, u32[]{:S(2)}) %collective-permute-start.4) | collective-permute-done | bytes 32800 | tf_op jit(solution)/shard_map/ppermute | solution.py:242
  53.6 1.0 %collective-permute-done.3 = bf16[2,2,16,256]{3,2,1,0:T(8,128)(2,1)S(1)} collective-permute-done((bf16[2,2,16,256]{3,2,1,0:T(8,128)(2,1)S(1)}, bf16[2,2,16,256]{3,2,1,0:T(8,128)(2,1)S(1)}, u32[]{:S(2)}, u32[]{:S(2)}) %collective-permute-start.3) | collective-permute-done | bytes 32800 | tf_op jit(solution)/shard_map/ppermute | solution.py:242
  54.7 0.1 add_multiply_fusion
  54.8 0.6 %slice_bitcast_fusion = (f32[1,2,256,16]{2,3,1,0:T(8,128)}, f32[1,2,256,16]{2,3,1,0:T(8,128)}) fusion(f32[2,2,16,256]{3,2,1,0:T(8,128)S(1)} %add_multiply_fusion), kind=kLoop, calls=%fused_computation.1 | loop fusion | bytes 131072 | tf_op jit(solution)/shard_map/transpose | solution.py:254
  (2 shorter events, 0.0 us)
Async XLA Ops:
  20.4 19.7 %all-to-all-start = ((bf16[8,32,512]{2,1,0:T(8,128)(2,1)}), bf16[8,32,512]{2,1,0:T(8,128)(2,1)S(1)}, u32[]{:S(2)}, u32[]{:S(2)}) async-start(bf16[8,32,512]{2,1,0:T(8,128)(2,1)} %get-tuple-element.8), calls=%async_computation | async-start | bytes 524288 | tf_op jit(solution)/shard_map/all_to_all | solution.py:192
  23.9 0.7 %copy-start.1 = (s32[1,2]{1,0:T(1,128)S(1)}, s32[1,2]{1,0:T(1,128)}, u32[]{:S(2)}) copy-start(s32[1,2]{1,0:T(1,128)} %a_ref.3) | copy-start | bytes 28
  24.5 0.7 %copy-start.3 = (s32[1,2]{1,0:T(1,128)S(1)}, s32[1,2]{1,0:T(1,128)}, u32[]{:S(2)}) copy-start(s32[1,2]{1,0:T(1,128)} %b_ref.3) | copy-start | bytes 28
  25.7 5.4 %collective-permute-start.1 = (bf16[4,40,512]{2,1,0:T(8,128)(2,1)S(1)}, bf16[4,40,512]{2,1,0:T(8,128)(2,1)S(1)}, u32[]{:S(2)}, u32[]{:S(2)}) collective-permute-start(bf16[4,40,512]{2,1,0:T(8,128)(2,1)S(1)} %shard_map.87.rest_0_), channel_id=1, source_target_pairs={{0,2},{1,3},{2,0},{3,1},{4,6},{5,7},{6,4},{7,5},{8,10},{9,11},{10,... | collective-permute-start | bytes 491528 | tf_op jit(solution)/shard_map/ppermute | solution.py:208
  27.3 4.5 %collective-permute-start = (bf16[4,40,512]{2,1,0:T(8,128)(2,1)S(1)}, bf16[4,40,512]{2,1,0:T(8,128)(2,1)S(1)}, u32[]{:S(2)}, u32[]{:S(2)}) collective-permute-start(bf16[4,40,512]{2,1,0:T(8,128)(2,1)S(1)} %shard_map.87.rest_0_), channel_id=1, source_target_pairs={{0,1},{1,0},{2,3},{3,2},{4,5},{5,4},{6,7},{7,6},{8,9},{9,8},{10,11... | collective-permute-start | bytes 491528 | tf_op jit(solution)/shard_map/ppermute | solution.py:208
  31.1 1.4 %collective-permute-start.2 = (bf16[4,40,512]{2,1,0:T(8,128)(2,1)S(1)}, bf16[4,40,512]{2,1,0:T(8,128)(2,1)S(1)}, u32[]{:S(2)}, u32[]{:S(2)}) collective-permute-start(bf16[4,40,512]{2,1,0:T(8,128)(2,1)S(1)} %collective-permute-done.1.rest_2_), channel_id=1, source_target_pairs={{0,1},{1,0},{2,3},{3,2},{4,5},{5,4},{6,7},{7,6},{8,9},{9,8},{10,11... | collective-permute-start | bytes 491528 | tf_op jit(solution)/shard_map/ppermute | solution.py:208
  32.5 1.6 %copy-start = (bf16[1,2048,512]{2,1,0:T(8,128)(2,1)S(1)}, bf16[1,2048,512]{2,1,0:T(8,128)(2,1)}, u32[]{:S(2)}) copy-start(bf16[1,2048,512]{2,1,0:T(8,128)(2,1)} %param.10) | copy-start | bytes 6291460
  34.1 6.0 %copy-start.2 = (s32[1,2]{1,0:T(1,128)S(1)}, s32[1,2]{1,0:T(1,128)}, u32[]{:S(2)}) copy-start(s32[1,2]{1,0:T(1,128)} %a_ref.3) | copy-start | bytes 28
  34.1 6.0 %copy-start.4 = (s32[1,2]{1,0:T(1,128)S(1)}, s32[1,2]{1,0:T(1,128)}, u32[]{:S(2)}) copy-start(s32[1,2]{1,0:T(1,128)} %b_ref.3) | copy-start | bytes 28
  49.5 1.9 %collective-permute-start.5 = (bf16[2,2,16,256]{3,2,1,0:T(8,128)(2,1)S(1)}, bf16[2,2,16,256]{3,2,1,0:T(8,128)(2,1)S(1)}, u32[]{:S(2)}, u32[]{:S(2)}) collective-permute-start(bf16[2,2,16,256]{3,2,1,0:T(8,128)(2,1)S(1)} %get-tuple-element.13), channel_id=1, source_target_pairs={{0,1},{1,0},{2,3},{3,2},{4,5},{5,4},{6,7},{7,6},{8,9},{9,8},{10,11... | collective-permute-start | bytes 98312 | tf_op jit(solution)/shard_map/ppermute | solution.py:242
  49.7 3.9 %collective-permute-start.4 = (bf16[2,2,16,256]{3,2,1,0:T(8,128)(2,1)S(1)}, bf16[2,2,16,256]{3,2,1,0:T(8,128)(2,1)S(1)}, u32[]{:S(2)}, u32[]{:S(2)}) collective-permute-start(bf16[2,2,16,256]{3,2,1,0:T(8,128)(2,1)S(1)} %get-tuple-element.12), channel_id=1, source_target_pairs={{0,2},{1,3},{2,0},{3,1},{4,6},{5,7},{6,4},{7,5},{8,10},{9,11},{10,... | collective-permute-start | bytes 98312 | tf_op jit(solution)/shard_map/ppermute | solution.py:242
  51.3 3.4 %collective-permute-start.3 = (bf16[2,2,16,256]{3,2,1,0:T(8,128)(2,1)S(1)}, bf16[2,2,16,256]{3,2,1,0:T(8,128)(2,1)S(1)}, u32[]{:S(2)}, u32[]{:S(2)}) collective-permute-start(bf16[2,2,16,256]{3,2,1,0:T(8,128)(2,1)S(1)} %get-tuple-element.11), channel_id=1, source_target_pairs={{0,3},{1,2},{2,1},{3,0},{4,7},{5,6},{6,5},{7,4},{8,11},{9,10},{10,... | collective-permute-start | bytes 98312 | tf_op jit(solution)/shard_map/ppermute | solution.py:242

commit v4 on v3

--- a/solution.py
+++ b/solution.py
@@ -12,7 +12,13 @@
 BF16 = jnp.bfloat16
 
 
-def prepare_kernel(con_ref, exc_ref, val_ref, first_ref, second_ref):
+def prepare_kernel(
+    a_ref, b_ref, con_ref, exc_ref, val_ref, first_ref, second_ref, roles_ref
+):
+    slots = a_ref.shape[1]
+    for p in range(slots):
+        roles_ref[p] = a_ref[0, p]
+        roles_ref[slots + p] = b_ref[0, p]
     ncon = con_ref.shape[1]
     rows_dev = exc_ref.shape[1]
     step = con_ref.shape[2] // rows_dev
@@ -26,11 +32,9 @@
         second_ref[k] = val_ref[0]
 
 
-def pick_kernel(a_ref, b_ref, all_ref, out_ref):
-    slots = a_ref.shape[1]
-    for p in range(slots):
-        out_ref[p] = all_ref[a_ref[0, p]]
-        out_ref[slots + p] = all_ref[b_ref[0, p]]
+def pick_kernel(roles_ref, all_ref, out_ref):
+    for i in range(out_ref.shape[0]):
+        out_ref[i] = all_ref[roles_ref[i]]
 
 
 def nt(a, b):
@@ -90,7 +94,7 @@
 
 
 def main_kernel(
-    sizes, a_ref, b_ref, ids_ref, all_ref, screened_ref, *rest
+    sizes, roles_ref, ids_ref, all_ref, screened_ref, *rest
 ):
     shards, direct = sizes[4:]
     sizes = sizes[:4]
@@ -116,7 +120,7 @@
     order = (moved == dst).astype(BF16)
     for p in range(slots):
         pair_products(
-            all_ref[a_ref[0, p]].astype(F32), all_ref[b_ref[0, p]].astype(F32), vals_ref, 0
+            all_ref[roles_ref[p]].astype(F32), all_ref[roles_ref[slots + p]].astype(F32), vals_ref, 0
         )
         for way in range(2):
             who = slots + p if way == 0 else p
@@ -178,25 +182,26 @@
     split = shards // parts
     vmem = pl.BlockSpec(memory_space=pltpu.VMEM)
     smem = pl.BlockSpec(memory_space=pltpu.SMEM)
-    mine_con, mine_val = pl.pallas_call(
+    mine_con, mine_val, roles = pl.pallas_call(
         prepare_kernel,
         out_shape=(
             jax.ShapeDtypeStruct((groups, keep, mu_dev), BF16),
             jax.ShapeDtypeStruct((groups, nval, mu_dev), BF16),
+            jax.ShapeDtypeStruct((2 * slots,), jnp.int32),
         ),
-        in_specs=[vmem] * 3,
-        out_specs=(vmem, vmem),
+        in_specs=[smem] * 2 + [vmem] * 3,
+        out_specs=(vmem, vmem, smem),
         cost_estimate=pl.CostEstimate(flops=0, transcendentals=0, bytes_accessed=6 * 2**20),
-    )(wave_con, excite[0].T, wave_val)
+    )(pair_kpoint, pair_partner, wave_con, excite[0].T, wave_val)
     all_con = lax.all_to_all(mine_con, "kgrp", 0, 0, tiled=True)
     all_val = lax.all_to_all(mine_val, "kgrp", 0, 0, tiled=True)
     selected = pl.pallas_call(
         pick_kernel,
         out_shape=jax.ShapeDtypeStruct((2 * slots, keep, mu_dev), BF16),
-        in_specs=[smem, smem, vmem],
+        in_specs=[smem, vmem],
         out_specs=vmem,
         compiler_params=pltpu.CompilerParams(vmem_limit_bytes=8 * 2**20),
-    )(pair_kpoint, pair_partner, all_con)
+    )(roles, all_con)
     direct = split == 1 and shards & (shards - 1) == 0
     if direct:
         ids = lax.axis_index("scr") ^ jnp.arange(shards, dtype=jnp.int32)
@@ -226,7 +231,7 @@
     partial = pl.pallas_call(
         functools.partial(main_kernel, (slots, nval, ncon, nexc, shards, direct)),
         out_shape=(block,) * parts,
-        in_specs=[smem] * 3 + [vmem] * (2 + shards),
+        in_specs=[smem] * 2 + [vmem] * (2 + shards),
         out_specs=(vmem,) * parts,
         scratch_shapes=[
             pltpu.VMEM((parts,) + block.shape, BF16),
@@ -236,12 +241,13 @@
             pltpu.VMEM((npb * per, LANES), BF16),
         ],
         compiler_params=limit,
-    )(pair_kpoint, pair_partner, ids, all_val, screened, *gathered)
+    )(roles, ids, all_val, screened, *gathered)
     if direct:
-        taken = [partial[0]] + [
-            lax.ppermute(partial[m], "scr", [(i, i ^ m) for i in range(shards)])
-            for m in range(shards - 1, 0, -1)
-        ]
+        taken = [partial[0]]
+        for m in range(shards - 1, 0, -1):
+            taken.append(
+                lax.ppermute(partial[m], "scr", [(i, i ^ m) for i in range(shards)])
+            )
     else:
         sent = jnp.stack(partial).reshape(parts, slots, 2, nexc, split, rows_dev)
         sent = sent.transpose(0, 4, 1, 2, 3, 5).reshape(shards, slots, 2, nexc, rows_dev)

time: 55.8 us -> 55.2 us (0.989)
  local copies, waits for them, and re-layouts: 3.54 us -> 2.88 us
    unnamed x10 -> x6, local copies, waits for them, and re-layouts: 2.9 us -> 2.25 us
where the time goes in v4:
time: 55.2 us; the launch traced here: 54.7 us
  blocking collectives  18.2 us (33%)
  Pallas kernels  17.6 us (32%)
  waiting for transfers between devices  7.73 us (14%)
  starting transfers between devices  6.93 us (13%)
  local copies, waits for them, and re-layouts  2.88 us (5%)
  between operations  1.37 us (2%)
    all_to_all x1, blocking collectives, body(): all_con = lax.all_to_all(mine_con, 'kgrp', 0, 0, tiled=True)  18.2 us
    pallas_call x1, Pallas kernels, body(): pl.pallas_call(functools.partial(main_kernel, (slots, nval, ncon, nexc, s...  9.37 us
    pallas_call x1, Pallas kernels, body(): pl.pallas_call(functools.partial(screen_kernel, (slots, ncon, shards)), o...  5.97 us
    ppermute x3, waiting for transfers between devices, body(): lax.ppermute(found[m], 'scr', [(i, i ^ step) for i in range(shards)])  4.52 us
    all_to_all x1, starting transfers between devices, body(): all_val = lax.all_to_all(mine_val, 'kgrp', 0, 0, tiled=True)  3.41 us
    ppermute x3, waiting for transfers between devices, body(): lax.ppermute(partial[m], 'scr', [(i, i ^ m) for i in range(shards)])  3.21 us
    unnamed x6, local copies, waits for them, and re-layouts  2.25 us
    ppermute x3, starting transfers between devices, body(): lax.ppermute(partial[m], 'scr', [(i, i ^ m) for i in range(shards)])  1.93 us
  transfers between devices with their start and end apart: 7, of which 4 were waited for; matrix products, arithmetic and copies ran while one was open for 0% of the time, Pallas kernels for 12%

profile of v4, /device:TPU:0, one launch (start us, length us, event | category | flops | bytes accessed | tf_op | source)
XLA Modules:
  0.0 54.7 jit_solution(8032421294425933053)
XLA Ops:
  0.6 1.7 %shard_map.86 = (bf16[8,40,512]{2,1,0:T(8,128)(2,1)}, bf16[8,32,512]{2,1,0:T(8,128)(2,1)}, s32[4]{0:T(128)}) custom-call(s32[1,2]{1,0:T(1,128)} %a_ref.1, s32[1,2]{1,0:T(1,128)} %b_ref.1, bf16[1,32,512]{2,1,0:T(8,128)(2,1)} %con_ref.1, bf16[16,256]{1,0:T(8,128)(2,1)} %bitcast.15, bf16[1,32,512]{2,1,0:T(8,128)(2,1)} %val_ref.1), custom_call_target="tpu_custom_call" | custom-call | bytes 6291456 | tf_op jit(solution)/shard_map/pallas_call | solution.py:185
  2.3 18.2 %all_to_all.10.all_ref = bf16[8,40,512]{2,1,0:T(8,128)(2,1)S(1)} all-to-all(bf16[8,40,512]{2,1,0:T(8,128)(2,1)} %get-tuple-element.11), channel_id=1, replica_groups=mesh['kgrp'=8,'scr'=4] {'kgrp'}, dimensions={0} | all-to-all | bytes 655360 | tf_op jit(solution)/shard_map/all_to_all | solution.py:196
  20.5 3.4 %all-to-all-start = ((bf16[8,32,512]{2,1,0:T(8,128)(2,1)}), bf16[8,32,512]{2,1,0:T(8,128)(2,1)S(1)}, u32[]{:S(2)}, u32[]{:S(2)}) async-start(bf16[8,32,512]{2,1,0:T(8,128)(2,1)} %get-tuple-element.10), calls=%async_computation | async-start | bytes 524288 | tf_op jit(solution)/shard_map/all_to_all | solution.py:197
  23.9 0.0 copy-start.1
  23.9 0.6 %copy-done.1 = s32[4]{0:T(128)S(1)} copy-done((s32[4]{0:T(128)S(1)}, s32[4]{0:T(128)}, u32[]{:S(2)}) %copy-start.1) | copy-done | bytes 40
  24.6 0.6 %shard_map.87.rest_0_ = bf16[4,40,512]{2,1,0:T(8,128)(2,1)S(1)} custom-call(s32[4]{0:T(128)S(1)} %copy-done.1, bf16[8,40,512]{2,1,0:T(8,128)(2,1)S(1)} %all_to_all.10.all_ref), custom_call_target="tpu_custom_call" | custom-call | tf_op jit(solution)/shard_map/pallas_call | solution.py:198
  25.1 1.6 %collective-permute-start.1 = (bf16[4,40,512]{2,1,0:T(8,128)(2,1)S(1)}, bf16[4,40,512]{2,1,0:T(8,128)(2,1)S(1)}, u32[]{:S(2)}, u32[]{:S(2)}) collective-permute-start(bf16[4,40,512]{2,1,0:T(8,128)(2,1)S(1)} %shard_map.87.rest_0_), channel_id=1, source_target_pairs={{0,2},{1,3},{2,0},{3,1},{4,6},{5,7},{6,4},{7,5},{8,10},{9,11},{10,... | collective-permute-start | bytes 491528 | tf_op jit(solution)/shard_map/ppermute | solution.py:213
  26.7 0.0 collective-permute-start
  26.7 3.8 %collective-permute-done.1.rest_2_ = bf16[4,40,512]{2,1,0:T(8,128)(2,1)S(1)} collective-permute-done((bf16[4,40,512]{2,1,0:T(8,128)(2,1)S(1)}, bf16[4,40,512]{2,1,0:T(8,128)(2,1)S(1)}, u32[]{:S(2)}, u32[]{:S(2)}) %collective-permute-start.1) | collective-permute-done | bytes 163872 | tf_op jit(solution)/shard_map/ppermute | solution.py:213
  30.5 0.0 collective-permute-start.2
  31.2 0.0 collective-permute-done.rest_1_
  31.2 0.7 %collective-permute-done.2.rest_3_ = bf16[4,40,512]{2,1,0:T(8,128)(2,1)S(1)} collective-permute-done((bf16[4,40,512]{2,1,0:T(8,128)(2,1)S(1)}, bf16[4,40,512]{2,1,0:T(8,128)(2,1)S(1)}, u32[]{:S(2)}, u32[]{:S(2)}) %collective-permute-start.2) | collective-permute-done | bytes 163872 | tf_op jit(solution)/shard_map/ppermute | solution.py:213
  31.9 0.0 copy-start
  31.9 1.6 %copy-done = bf16[1,2048,512]{2,1,0:T(8,128)(2,1)S(1)} copy-done((bf16[1,2048,512]{2,1,0:T(8,128)(2,1)S(1)}, bf16[1,2048,512]{2,1,0:T(8,128)(2,1)}, u32[]{:S(2)}) %copy-start) | copy-done | bytes 2097176
  33.5 0.0 copy-start.2
  33.5 6.0 %shard_map.88.screened_ref = bf16[2,1024,512]{2,1,0:T(8,128)(2,1)S(1)} custom-call(s32[4]{0:T(128)S(1)} %iota_xor_fusion.ids_ref, bf16[2048,512]{1,0:T(8,128)(2,1)S(1)} %bitcast.14, bf16[4,40,512]{2,1,0:T(8,128)(2,1)S(1)} %shard_map.87.rest_0_, bf16[4,40,512]{2,1,0:T(8,128)(2,1)S(1)} %collective-permute-done.rest_1_, ...), custom_call_target="tpu_custom_call" | custom-call | tf_op jit(solution)/shard_map/pallas_call | solution.py:223
  39.5 0.0 all-to-all-done.all_ref
  39.5 0.0 copy-done.2
  39.5 9.4 %shard_map.89 = (bf16[2,2,16,256]{3,2,1,0:T(8,128)(2,1)S(1)}, bf16[2,2,16,256]{3,2,1,0:T(8,128)(2,1)S(1)}, bf16[2,2,16,256]{3,2,1,0:T(8,128)(2,1)S(1)}, bf16[2,2,16,256]{3,2,1,0:T(8,128)(2,1)S(1)}) custom-call(s32[4]{0:T(128)S(1)} %copy-done.2, s32[4]{0:T(128)S(1)} %iota_xor_fusion.ids_ref, bf16[8,32,512]{2,1,0:T(8,128)(2,1)S(1)} %all-to-all-done.all_ref, ...), custom_call_target="tpu_custom_call" | custom-call | tf_op jit(solution)/shard_map/pallas_call | solution.py:231
  48.9 0.2 collective-permute-start.5
  49.1 1.5 %collective-permute-start.4 = (bf16[2,2,16,256]{3,2,1,0:T(8,128)(2,1)S(1)}, bf16[2,2,16,256]{3,2,1,0:T(8,128)(2,1)S(1)}, u32[]{:S(2)}, u32[]{:S(2)}) collective-permute-start(bf16[2,2,16,256]{3,2,1,0:T(8,128)(2,1)S(1)} %get-tuple-element.14), channel_id=1, source_target_pairs={{0,2},{1,3},{2,0},{3,1},{4,6},{5,7},{6,4},{7,5},{8,10},{9,11},{10,... | collective-permute-start | bytes 98312 | tf_op jit(solution)/shard_map/ppermute | solution.py:249
  50.6 0.2 collective-permute-start.3
  50.8 0.0 collective-permute-done.5
  50.8 2.2 %collective-permute-done.4 = bf16[2,2,16,256]{3,2,1,0:T(8,128)(2,1)S(1)} collective-permute-done((bf16[2,2,16,256]{3,2,1,0:T(8,128)(2,1)S(1)}, bf16[2,2,16,256]{3,2,1,0:T(8,128)(2,1)S(1)}, u32[]{:S(2)}, u32[]{:S(2)}) %collective-permute-start.4) | collective-permute-done | bytes 32800 | tf_op jit(solution)/shard_map/ppermute | solution.py:249
  53.0 1.0 %collective-permute-done.3 = bf16[2,2,16,256]{3,2,1,0:T(8,128)(2,1)S(1)} collective-permute-done((bf16[2,2,16,256]{3,2,1,0:T(8,128)(2,1)S(1)}, bf16[2,2,16,256]{3,2,1,0:T(8,128)(2,1)S(1)}, u32[]{:S(2)}, u32[]{:S(2)}) %collective-permute-start.3) | collective-permute-done | bytes 32800 | tf_op jit(solution)/shard_map/ppermute | solution.py:249
  54.0 0.1 add_multiply_fusion
  54.1 0.6 %slice_bitcast_fusion = (f32[1,2,256,16]{2,3,1,0:T(8,128)}, f32[1,2,256,16]{2,3,1,0:T(8,128)}) fusion(f32[2,2,16,256]{3,2,1,0:T(8,128)S(1)} %add_multiply_fusion), kind=kLoop, calls=%fused_computation.1 | loop fusion | bytes 131072 | tf_op jit(solution)/shard_map/transpose | solution.py:260
  (2 shorter events, 0.0 us)
Async XLA Ops:
  20.5 19.0 %all-to-all-start = ((bf16[8,32,512]{2,1,0:T(8,128)(2,1)}), bf16[8,32,512]{2,1,0:T(8,128)(2,1)S(1)}, u32[]{:S(2)}, u32[]{:S(2)}) async-start(bf16[8,32,512]{2,1,0:T(8,128)(2,1)} %get-tuple-element.10), calls=%async_computation | async-start | bytes 524288 | tf_op jit(solution)/shard_map/all_to_all | solution.py:197
  23.9 0.7 %copy-start.1 = (s32[4]{0:T(128)S(1)}, s32[4]{0:T(128)}, u32[]{:S(2)}) copy-start(s32[4]{0:T(128)} %get-tuple-element.9.roles_ref) | copy-start | bytes 52
  25.1 5.4 %collective-permute-start.1 = (bf16[4,40,512]{2,1,0:T(8,128)(2,1)S(1)}, bf16[4,40,512]{2,1,0:T(8,128)(2,1)S(1)}, u32[]{:S(2)}, u32[]{:S(2)}) collective-permute-start(bf16[4,40,512]{2,1,0:T(8,128)(2,1)S(1)} %shard_map.87.rest_0_), channel_id=1, source_target_pairs={{0,2},{1,3},{2,0},{3,1},{4,6},{5,7},{6,4},{7,5},{8,10},{9,11},{10,... | collective-permute-start | bytes 491528 | tf_op jit(solution)/shard_map/ppermute | solution.py:213
  26.7 4.5 %collective-permute-start = (bf16[4,40,512]{2,1,0:T(8,128)(2,1)S(1)}, bf16[4,40,512]{2,1,0:T(8,128)(2,1)S(1)}, u32[]{:S(2)}, u32[]{:S(2)}) collective-permute-start(bf16[4,40,512]{2,1,0:T(8,128)(2,1)S(1)} %shard_map.87.rest_0_), channel_id=1, source_target_pairs={{0,1},{1,0},{2,3},{3,2},{4,5},{5,4},{6,7},{7,6},{8,9},{9,8},{10,11... | collective-permute-start | bytes 491528 | tf_op jit(solution)/shard_map/ppermute | solution.py:213
  30.5 1.4 %collective-permute-start.2 = (bf16[4,40,512]{2,1,0:T(8,128)(2,1)S(1)}, bf16[4,40,512]{2,1,0:T(8,128)(2,1)S(1)}, u32[]{:S(2)}, u32[]{:S(2)}) collective-permute-start(bf16[4,40,512]{2,1,0:T(8,128)(2,1)S(1)} %collective-permute-done.1.rest_2_), channel_id=1, source_target_pairs={{0,1},{1,0},{2,3},{3,2},{4,5},{5,4},{6,7},{7,6},{8,9},{9,8},{10,11... | collective-permute-start | bytes 491528 | tf_op jit(solution)/shard_map/ppermute | solution.py:213
  31.9 1.6 %copy-start = (bf16[1,2048,512]{2,1,0:T(8,128)(2,1)S(1)}, bf16[1,2048,512]{2,1,0:T(8,128)(2,1)}, u32[]{:S(2)}) copy-start(bf16[1,2048,512]{2,1,0:T(8,128)(2,1)} %param.10) | copy-start | bytes 6291460
  33.5 6.0 %copy-start.2 = (s32[4]{0:T(128)S(1)}, s32[4]{0:T(128)}, u32[]{:S(2)}) copy-start(s32[4]{0:T(128)} %get-tuple-element.9.roles_ref) | copy-start | bytes 52
  48.9 1.9 %collective-permute-start.5 = (bf16[2,2,16,256]{3,2,1,0:T(8,128)(2,1)S(1)}, bf16[2,2,16,256]{3,2,1,0:T(8,128)(2,1)S(1)}, u32[]{:S(2)}, u32[]{:S(2)}) collective-permute-start(bf16[2,2,16,256]{3,2,1,0:T(8,128)(2,1)S(1)} %get-tuple-element.15), channel_id=1, source_target_pairs={{0,1},{1,0},{2,3},{3,2},{4,5},{5,4},{6,7},{7,6},{8,9},{9,8},{10,11... | collective-permute-start | bytes 98312 | tf_op jit(solution)/shard_map/ppermute | solution.py:249
  49.1 3.9 %collective-permute-start.4 = (bf16[2,2,16,256]{3,2,1,0:T(8,128)(2,1)S(1)}, bf16[2,2,16,256]{3,2,1,0:T(8,128)(2,1)S(1)}, u32[]{:S(2)}, u32[]{:S(2)}) collective-permute-start(bf16[2,2,16,256]{3,2,1,0:T(8,128)(2,1)S(1)} %get-tuple-element.14), channel_id=1, source_target_pairs={{0,2},{1,3},{2,0},{3,1},{4,6},{5,7},{6,4},{7,5},{8,10},{9,11},{10,... | collective-permute-start | bytes 98312 | tf_op jit(solution)/shard_map/ppermute | solution.py:249
  50.6 3.4 %collective-permute-start.3 = (bf16[2,2,16,256]{3,2,1,0:T(8,128)(2,1)S(1)}, bf16[2,2,16,256]{3,2,1,0:T(8,128)(2,1)S(1)}, u32[]{:S(2)}, u32[]{:S(2)}) collective-permute-start(bf16[2,2,16,256]{3,2,1,0:T(8,128)(2,1)S(1)} %get-tuple-element.13), channel_id=1, source_target_pairs={{0,3},{1,2},{2,1},{3,0},{4,7},{5,6},{6,5},{7,4},{8,11},{9,10},{10,... | collective-permute-start | bytes 98312 | tf_op jit(solution)/shard_map/ppermute | solution.py:249
